TPU v7x, 32 devices: a whole 2x2x4 slice. The times are simulated.
32 devices in a mesh: pop: 8 (over z, y), tp: 4 (over x, core).
Axes of the slice: x: 2, y: 2, z: 4, core: 2. Of those that a mesh axis runs over, the one named last changes fastest.
Arguments:
- tokens: bfloat16 [8192, 5120], P('pop', 'tp'), may hold values from -6 to 6
- target: bfloat16 [8192, 5120], P('pop', 'tp'), may hold values from -6 to 6
- weight: bfloat16 [5120, 5120], P('pop', 'tp'), may hold values from -6 to 6
- factor_out: bfloat16 [32, 4, 5120], P('pop'), may hold values from -6 to 6
- factor_in: bfloat16 [32, 4, 5120], P('pop', None, 'tp'), may hold values from -6 to 6
Outputs:
- perturbed: bfloat16 [8192, 5120], P('pop', 'tp')
- new_weight: bfloat16 [5120, 5120], P('pop', 'tp')
All inputs are finite; a program needn't handle non-finite values.
Results may differ from a plain program's by a relative error of at most 0.012.
Values may be sent and summed in bfloat16 or wider, within the bound.
No kernel may reach another device: no remote copies, remote signals or barrier semaphores. Data moves between devices by JAX's collectives and lax.ppermute only.
A program may use at most 128 MiB of HBM per device.

v0:
```python
import math

import jax
import jax.numpy as jnp
from jax import lax
from jax.sharding import PartitionSpec as P

noise_scale = 0.25
step_scale = 10.0


def local(tokens, target, weight, factor_out, factor_in):
    tok_rows, shard_width = tokens.shape
    mem_local, rank, width_out = factor_out.shape
    tok_member = tok_rows // mem_local
    tp_count = lax.axis_size("tp")
    width_in = shard_width * tp_count
    out_cols = width_out // tp_count
    col_first = lax.axis_index("tp") * out_cols
    base_factor = 1.0 / math.sqrt(width_in)
    token_sets = tokens.reshape(mem_local, tok_member, shard_width)
    codes_part = jnp.einsum(
        "mkc,mrc->mkr", token_sets, factor_in, preferred_element_type=jnp.float32
    )
    codes_sum = lax.psum(codes_part, "tp")
    partial_terms = (
        lax.dot_general(
            tokens,
            lax.all_gather(weight, "pop", axis=0, tiled=True),
            (((1,), (1,)), ((), ())),
            preferred_element_type=jnp.float32,
        )
        * base_factor
    )
    base_sum = lax.psum_scatter(
        partial_terms.astype(jnp.bfloat16), "tp", scatter_dimension=1, tiled=True
    ).astype(jnp.float32)
    outer_cols = lax.dynamic_slice_in_dim(factor_out, col_first, out_cols, 2).astype(jnp.float32)
    low_rank = jnp.einsum(
        "mkr,mrc->mkc", codes_sum, outer_cols, precision=lax.Precision.HIGHEST
    ) * (noise_scale / math.sqrt(rank * width_in))
    output_full = base_sum.reshape(mem_local, tok_member, out_cols) + low_rank
    wanted = target.reshape(mem_local, tok_member, out_cols).astype(jnp.float32)
    fitness_part = jnp.sum(output_full * wanted, axis=(1, 2)) / (tok_member * math.sqrt(width_out))
    fitness_local = lax.psum(fitness_part, "tp")
    fitness_all = lax.all_gather(fitness_local, "pop", axis=0, tiled=True)
    outer_rows = lax.all_to_all(factor_out, "pop", split_axis=2, concat_axis=0, tiled=True)
    inner_cols = lax.all_gather(factor_in, "pop", axis=0, tiled=True)
    centered = fitness_all - jnp.mean(fitness_all)
    scaled = (centered[:, None, None] * outer_rows.astype(jnp.float32)).astype(jnp.bfloat16)
    delta = jnp.einsum("imo,imc->oc", scaled, inner_cols, preferred_element_type=jnp.float32)
    members_all = fitness_all.shape[0]
    updated = (
        weight.astype(jnp.float32) + step_scale / math.sqrt(members_all * rank) * delta
    ).astype(jnp.bfloat16)
    return (output_full.reshape(tok_rows, out_cols).astype(jnp.bfloat16), updated)


def solution(mesh):
    in_specs = (
        P("pop", "tp"),
        P("pop", "tp"),
        P("pop", "tp"),
        P("pop", None, None),
        P("pop", None, "tp"),
    )
    out_specs = (P("pop", "tp"), P("pop", "tp"))
    return jax.shard_map(local, mesh=mesh, in_specs=in_specs, out_specs=out_specs, check_vma=False)
```

profile of v0, /device:TPU:0, one launch (start us, length us, event | category | flops | bytes accessed | tf_op | source)
XLA Modules:
  0.0 356.7 jit_solution(14333181768986862038)
XLA Ops:
  7.2 0.0 copy-start
  7.2 0.0 all-gather.2.cloned.1.call-start
  7.2 0.7 all-gather.2.cloned.1.call-update
  7.9 0.0 reduce-scatter.2.cloned.1.call-start
  8.0 187.5 %all-gather.2.cloned.1.call-done = bf16[5120,1280]{1,0:T(8,128)(2,1)} async-done(((bf16[640,1280]{1,0:T(8,128)(2,1)}), bf16[5120,1280]{1,0:T(8,128)(2,1)}) %all-gather.2.cloned.1.call-update) | async-done | bytes 13107216 | tf_op jit(solution)/shard_map/all_gather | solution.py:29
  195.4 0.0 copy-done
  195.4 20.6 %multiply_convert_fusion = bf16[1024,5120]{1,0:T(8,128)(2,1)} fusion(bf16[1024,1280]{1,0:T(8,128)(2,1)S(1)} %copy-done, bf16[5120,1280]{1,0:T(8,128)(2,1)} %all-gather.2.cloned.1.call-done), kind=kOutput, calls=%fused_computation | convolution fusion | flops 13432258560 | bytes 26214400 | tf_op jit(solution)/shard_map/dot_general | solution.py:27
  216.0 0.0 copy-start.1
  216.0 0.0 reduce-scatter.2.cloned.1.call-update
  216.1 0.9 copy-done.1
  217.0 5.2 %copy.9 = bf16[4,4,5120]{1,0,2:T(4,128)(2,1)} copy(bf16[4,4,5120]{2,1,0:T(4,128)(2,1)S(1)} %copy-done.1) | data formatting | bytes 327680 | tf_op args[3]
  222.2 0.0 copy-start.2
  222.2 0.0 copy-start.3
  222.2 12.0 %reshape.37 = bf16[8,2,5120]{2,1,0:T(2,128)(2,1)} reshape(bf16[5120,4,4]{2,1,0:T(4,128)(2,1)} %bitcast.29) | data formatting | bytes 327680
  234.2 3.4 all-to-all-start
  237.6 0.0 copy-done.2
  237.6 0.8 fusion.8
  238.4 0.0 copy-done.3
  238.4 0.6 dynamic-slice
  239.6 11.8 %psum.14 = f32[4,256,4]{1,2,0:T(4,128)S(1)} all-reduce(f32[4,256,4]{1,2,0:T(4,128)S(1)} %fusion.8), channel_id=1, replica_groups=mesh['pop'=8,'tp'=4] {'tp'}, use_global_device_ids=true, to_apply=%region_1.0 | all-reduce | flops 4096 | bytes 32768 | tf_op jit(solution)/shard_map/psum | solution.py:25
  251.4 31.6 %all_gather.11 = bf16[32,4,1280]{2,1,0:T(4,128)(2,1)S(1)} all-gather(bf16[4,4,1280]{2,1,0:T(4,128)(2,1)S(1)} %copy-done.2), channel_id=1, replica_groups=mesh['pop'=8,'tp'=4] {'pop'}, dimensions={0}, use_global_device_ids=true | all-gather | bytes 368640 | tf_op jit(solution)/shard_map/all_gather | solution.py:48
  283.0 0.0 all-to-all-done
  283.0 12.3 %reshape.38 = bf16[5120,4,4]{2,1,0:T(4,128)(2,1)} reshape(bf16[8,2,5120]{2,1,0:T(2,128)(2,1)S(1)} %all-to-all-done) | data formatting | bytes 327680
  295.3 7.2 %convert_bitcast_fusion = f32[8,4,4,640]{2,1,3,0:T(4,128)} fusion(bf16[4,4,8,640]{1,0,3,2:T(4,128)(2,1)} %bitcast.30), kind=kLoop, calls=%fused_computation.1 | loop fusion | flops 81920 | bytes 491520 | tf_op jit(solution)/shard_map/convert_element_type | solution.py:50
  302.5 7.6 %copy.10 = f32[8,4,4,640]{3,1,0,2:T(4,128)S(1)} copy(f32[8,4,4,640]{2,1,3,0:T(4,128)} %convert_bitcast_fusion) | data formatting | bytes 655360 | tf_op jit(solution)/shard_map/convert_element_type | solution.py:50
  310.1 0.0 reduce-scatter.2.cloned.1.call-done
  310.1 7.2 %fusion = (f32[4]{0:T(128)S(1)}, bf16[4,256,1280]{2,1,0:T(8,128)(2,1)}) fusion(bf16[4,256,1280]{2,1,0:T(8,128)(2,1)} %bitcast.31, f32[4,256,4]{1,2,0:T(4,128)S(1)} %psum.14, bf16[4,4,5120]{2,1,0:T(4,128)(2,1)S(1)} %copy-done.1, s32[]{:T(128)S(6)} %select_n.3, bf16[4,256,1280]{2,1,0:T(8,128)(2,1)} %bitcast.32), kind=kOutput, calls=%fused_computation.3 | convolution fusion | flops 72089600 | bytes 7921684 | tf_op jit(solution)/shard_map/mkr,mrc->mkc/dot_general | solution.py:39
  317.3 0.8 reshape.29
  318.1 5.6 %psum.15 = f32[4]{0:T(128)S(1)} all-reduce(f32[4]{0:T(128)S(1)} %broadcast_multiply_fusion), channel_id=1, replica_groups=mesh['pop'=8,'tp'=4] {'tp'}, use_global_device_ids=true, to_apply=%region_3.0 | all-reduce | flops 4 | bytes 32 | tf_op jit(solution)/shard_map/psum | solution.py:45
  323.7 0.2 dynamic-update-slice
  324.0 21.2 %all-reduce = f32[32]{0:T(128)S(1)} all-reduce(f32[32]{0:T(128)S(1)} %dynamic-update-slice), channel_id=1, replica_groups=mesh['pop'=8,'tp'=4] {'pop'}, use_global_device_ids=true, to_apply=%add | all-reduce | flops 32 | bytes 256
  345.2 0.6 reduce_sum.19
  346.4 3.4 fusion.3
  (3 shorter events, 0.0 us)
Async XLA Ops:
  7.2 188.3 %copy-start = (bf16[1024,1280]{1,0:T(8,128)(2,1)S(1)}, bf16[1024,1280]{1,0:T(8,128)(2,1)}, u32[]{:S(2)}) copy-start(bf16[1024,1280]{1,0:T(8,128)(2,1)} %param.5) | copy-start | bytes 7864324
  7.2 188.2 %all-gather.2.cloned.1.call-start = ((), (), s32[]{:S(2)}) async-start(), calls=%async_computation.2 | async-start | bytes 14745600 | tf_op jit(solution)/shard_map/all_gather | solution.py:29
  7.9 302.2 %reduce-scatter.2.cloned.1.call-start = ((), (), s32[]{:S(2)}) async-start(), calls=%async_computation.3 | async-start | bytes 13107200 | tf_op jit(solution)/shard_map/reduce_scatter | solution.py:35
  216.0 0.9 copy-start.1
  222.2 15.4 %copy-start.2 = (bf16[4,4,1280]{2,1,0:T(4,128)(2,1)S(1)}, bf16[4,4,1280]{2,1,0:T(4,128)(2,1)}, u32[]{:S(2)}) copy-start(bf16[4,4,1280]{2,1,0:T(4,128)(2,1)} %param.9) | copy-start | bytes 122884
  222.2 16.2 %copy-start.3 = (u32[32]{0:T(128)S(1)}, u32[32]{0:T(128)}, u32[]{:S(2)}) copy-start(u32[32]{0:T(128)} %constant.28) | copy-start | bytes 388
  234.2 48.8 %all-to-all-start = ((bf16[8,2,5120]{2,1,0:T(2,128)(2,1)}), bf16[8,2,5120]{2,1,0:T(2,128)(2,1)S(1)}, u32[]{:S(2)}, u32[]{:S(2)}) async-start(bf16[8,2,5120]{2,1,0:T(2,128)(2,1)} %reshape.37), calls=%async_computation.1 | async-start | bytes 327680 | tf_op jit(solution)/shard_map/all_to_all | solution.py:47
Sparse Core Ops, SparseCore 0:
  10.2 185.2 all-gather.1
  216.2 82.6 reduce-scatter.1
where the time goes:
time: 357 us
  waiting for transfers between devices  188 us (53%)
  blocking collectives  70.2 us (20%)
  local copies, waits for them, and re-layouts  39.7 us (11%)
  matrix products  32 us (9%)
  between operations  15.4 us (4%)
  other arithmetic  7.78 us (2%)
    all_gather x1, waiting for transfers between devices, local(): lax.all_gather(weight, 'pop', axis=0, tiled=True)  187 us
    all_gather x1, blocking collectives, local(): inner_cols = lax.all_gather(factor_in, 'pop', axis=0, tiled=True)  31.6 us
    unnamed x14, local copies, waits for them, and re-layouts  31.3 us
    unnamed x1, blocking collectives  21.2 us
    dot_general x1, matrix products, local(): lax.dot_general(tokens, lax.all_gather(weight, 'pop', axis=0, tiled=True)...  20.6 us
    psum x1, blocking collectives, local(): codes_sum = lax.psum(codes_part, 'tp')  11.8 us
    convert_element_type x2, local copies, waits for them, and re-layouts, local(): outer_rows.astype(jnp.float32)  8.41 us
    dot_general x1, matrix products, local(): jnp.einsum('mkr,mrc->mkc', codes_sum, outer_cols, precision=lax.Precision...  7.17 us
  transfers between devices with their start and end apart: 3, of which 1 were waited for; matrix products, arithmetic and copies ran while one was open for 13% of the time, Pallas kernels for 0%

commit v1 on v0

--- a/solution.py
+++ b/solution.py
@@ -3,13 +3,20 @@
 import jax
 import jax.numpy as jnp
 from jax import lax
+from jax.experimental import pallas as pl
+from jax.experimental.pallas import tpu as pltpu
 from jax.sharding import PartitionSpec as P
+
 
 noise_scale = 0.25
 step_scale = 10.0
 
-
-def local(tokens, target, weight, factor_out, factor_in):
+AXES = ("pop", "tp")
+LINE = 4
+LANES = 128
+
+
+def plain(tokens, target, weight, factor_out, factor_in):
     tok_rows, shard_width = tokens.shape
     mem_local, rank, width_out = factor_out.shape
     tok_member = tok_rows // mem_local
@@ -56,6 +63,234 @@
     return (output_full.reshape(tok_rows, out_cols).astype(jnp.bfloat16), updated)
 
 
+def send(array, rule):
+    pairs = []
+    for z in range(LINE):
+        for y in range(2):
+            for x in range(2):
+                for c in range(2):
+                    to = rule(z, y, x, c)
+                    if to is not None:
+                        tz, ty, tx, tc = to
+                        pairs.append(
+                            (((z * 2 + y) * 2 + x) * 2 + c, ((tz * 2 + ty) * 2 + tx) * 2 + tc)
+                        )
+    return lax.ppermute(array, AXES, pairs)
+
+
+def keep_core(z, x, step):
+    return ((z % 2) if x == z // 2 else (z // 2)) ^ step
+
+
+def cuts(rows):
+    blocks = rows // LANES
+    wide = max(1, (blocks - 1) // 2)
+    edges = sorted({0, wide * LANES, (blocks - 1) * LANES, blocks * LANES})
+    return tuple(zip(edges[:-1], edges[1:]))
+
+
+def contract(left, right):
+    return lax.dot_general(left, right, (((1,), (1,)), ((), ())), preferred_element_type=jnp.float32)
+
+
+def finish_body(count, flags, *refs):
+    totals, sides, others = (refs[2 * count * g : 2 * count * (g + 1)] for g in range(3))
+    low_ref, want_ref, out_ref, fit_ref = refs[6 * count :]
+    half = pl.program_id(1)
+
+    def emit(group):
+        base = jnp.concatenate([ref[...] for ref in group], axis=1)
+        value = base.astype(jnp.float32) + low_ref[...]
+        out_ref[...] = value.astype(out_ref.dtype)
+        product = value * want_ref[...].astype(jnp.float32)
+        rows, cols = product.shape
+        folded = product.reshape(rows // 8, 8, cols).sum(axis=0)
+        lanes = sum(folded[:, lo : lo + LANES] for lo in range(0, cols, LANES))
+
+        @pl.when(half == 0)
+        def _():
+            fit_ref[0] = lanes
+
+        @pl.when(half == 1)
+        def _():
+            fit_ref[0] += lanes
+
+    for step in range(2):
+        here = flags[0] == step
+        part = slice(step * count, (step + 1) * count)
+
+        @pl.when(here & (half == 0) & (flags[1] == 0))
+        def _():
+            emit(totals[part])
+
+        @pl.when(here & (half == 0) & (flags[1] == 1))
+        def _():
+            emit(sides[part])
+
+        @pl.when(here & (half == 1))
+        def _():
+            emit(others[part])
+
+
+def finish(flags, totals, sides, others, low_rank, target, members):
+    rows, width = low_rank.shape
+    block = rows // members
+    count = len(totals) // 2
+
+    def column(m, h, flags):
+        own = flags[2]
+        return (m, jnp.where(h == 0, own, 1 - own))
+
+    def spec(array, want):
+        return pl.BlockSpec(
+            (block, array.shape[1]), lambda m, h, flags: (jnp.where(want(flags), m, 0), 0)
+        )
+
+    specs = []
+    for group, side in ((totals, 0), (sides, 1), (others, None)):
+        for i, array in enumerate(group):
+            step = i // count
+            if side is None:
+                specs.append(spec(array, lambda f, s=step: f[0] == s))
+            else:
+                specs.append(spec(array, lambda f, s=step, d=side: (f[0] == s) & (f[1] == d)))
+    specs += [pl.BlockSpec((block, width // 2), column)] * 2
+    return pl.pallas_call(
+        lambda flags, *refs: finish_body(count, flags, *refs),
+        grid_spec=pltpu.PrefetchScalarGridSpec(
+            num_scalar_prefetch=1,
+            grid=(members, 2),
+            in_specs=specs,
+            out_specs=[
+                pl.BlockSpec((block, width // 2), column),
+                pl.BlockSpec((1, 8, LANES), lambda m, h, flags: (m, 0, 0)),
+            ],
+        ),
+        out_shape=[
+            jax.ShapeDtypeStruct((rows, width), target.dtype),
+            jax.ShapeDtypeStruct((members, 8, LANES), jnp.float32),
+        ],
+        cost_estimate=pl.CostEstimate(
+            flops=4 * rows * width, bytes_accessed=12 * rows * width, transcendentals=0
+        ),
+        compiler_params=pltpu.CompilerParams(vmem_limit_bytes=16 * 1024 * 1024),
+    )(flags, *totals, *sides, *others, low_rank, target)
+
+
+def local(tokens, target, weight, factor_out, factor_in):
+    return split_step(tokens, target, weight, factor_out, factor_in)
+
+
+def split_step(tokens, target, weight, factor_out, factor_in):
+    tok_rows, shard_width = tokens.shape
+    mem_local, rank, width_out = factor_out.shape
+    weight_rows = weight.shape[0]
+    tok_member = tok_rows // mem_local
+    tp_count = lax.axis_size("tp")
+    pop_count = lax.axis_size("pop")
+    width_in = shard_width * tp_count
+    out_cols = width_out // tp_count
+    base_factor = 1.0 / math.sqrt(width_in)
+    pop, tp = lax.axis_index("pop"), lax.axis_index("tp")
+    z, y, x, c = pop // 2, pop % 2, tp // 2, tp % 2
+    inner = (z == 1) | (z == 2)
+    near_first = x == z // 2
+    bit = jnp.where(near_first, z % 2, z // 2)
+    flags = jnp.stack([c ^ bit, c, y]).astype(jnp.int32)
+    pieces = cuts(weight_rows)
+    count = len(pieces)
+    sub = lambda array: [array[lo:hi] for lo, hi in pieces]
+
+    partner = lambda z, y, x, c: (z, y, x, 1 - c)
+
+    mid = lambda z, y, x, c: (3 - z, y, x, c) if z in (1, 2) else None
+    end = lambda z, y, x, c: (z ^ 1, y, x, c) if z in (1, 2) else None
+    swap = send(weight, lambda z, y, x, c: (z ^ 1, y, x, c))
+    early = [lax.optimization_barrier(sub(weight)), lax.optimization_barrier(sub(swap))]
+    early_o = [send(weight, partner), send(swap, partner)]
+    rows_a = send(tokens, lambda z, y, x, c: (z, 1 - y, x, 1) if c == 0 else None)
+    rows_p = send(tokens, partner)
+    rows_b = send(tokens, lambda z, y, x, c: (z, 1 - y, x, 1) if c == 1 else None)
+    at_mid = [[send(early[s][k], mid) for k in range(count)] for s in range(2)]
+    at_end = [[send(at_mid[s][k], end) for k in range(count)] for s in range(2)]
+    rows_a, rows_b = jnp.where(c == 0, rows_p, rows_a), jnp.where(c == 0, tokens, rows_b)
+
+    outer_flat = factor_out.reshape(mem_local * rank, width_out)
+    inner_flat = factor_in.reshape(mem_local * rank, shard_width)
+    payload = jnp.concatenate(
+        [
+            outer_flat.reshape(mem_local * rank, pop_count, weight_rows).transpose(1, 0, 2),
+            jnp.broadcast_to(inner_flat[None], (pop_count,) + inner_flat.shape),
+        ],
+        axis=2,
+    )
+    factors = lax.all_to_all(payload, "pop", split_axis=0, concat_axis=0, tiled=True)
+    factors = factors.reshape(pop_count * mem_local * rank, weight_rows + shard_width)
+
+    token_sets = tokens.reshape(mem_local, tok_member, shard_width)
+    codes = jnp.einsum("mkc,mrc->mrk", token_sets, factor_in, preferred_element_type=jnp.float32)
+    codes = codes.reshape(mem_local * rank, tok_member)
+    codes = codes + send(codes, lambda z, y, x, c: (z, y, x, 1 - c))
+    codes = codes + send(codes, lambda z, y, x, c: (z, y, 1 - x, c))
+    codes = codes.reshape(mem_local, rank, tok_member)
+    outer_cols = lax.dynamic_slice_in_dim(factor_out, tp * out_cols, out_cols, 2).astype(jnp.float32)
+    low_rank = jnp.einsum(
+        "mrk,mrc->mkc", codes, outer_cols, precision=lax.Precision.HIGHEST
+    ) * (noise_scale / math.sqrt(rank * width_in))
+    low_rank = low_rank.reshape(tok_rows, out_cols)
+
+    rows_a, rows_b, low_rank, factors = lax.optimization_barrier((rows_a, rows_b, low_rank, factors))
+    outer_rows, inner_cols = factors[:, :weight_rows], factors[:, weight_rows:]
+    early_sum = [[None] * count, [None] * count]
+    for step in range(2):
+        for k, (lo, hi) in enumerate(pieces):
+            early_sum[step][k] = contract(rows_b, early[step][k]) + contract(
+                rows_a, early_o[step][lo:hi]
+            )
+    totals, sides, others = [], [], []
+    for step in range(2):
+        for k in range(count):
+            last = jnp.where(inner, at_mid[step][k], at_end[step][k])
+            last_o = send(last, partner)
+            last_sum = contract(rows_b, last) + contract(rows_a, last_o)
+            far_sum = jnp.where(near_first, last_sum, early_sum[step][k]) * base_factor
+            near_sum = jnp.where(near_first, early_sum[step][k], last_sum) * base_factor
+            far_sum = far_sum.astype(jnp.bfloat16)
+            moved = send(far_sum, lambda z, y, x, c: (z, y, 1 - x, c))
+            total = (near_sum + moved.astype(jnp.float32)).astype(jnp.bfloat16)
+            totals.append(total)
+            sides.append(send(total, partner))
+            others.append(
+                send(
+                    total,
+                    lambda z, y, x, c: (z, 1 - y, x, keep_core(z, x, step)) if c == 1 else None,
+                )
+            )
+
+    out, fits = finish(flags, totals, sides, others, low_rank, target, mem_local)
+    fitness_part = jnp.sum(fits, axis=(1, 2)) / (tok_member * math.sqrt(width_out))
+    members_all = pop_count * mem_local
+    slots = jnp.arange(members_all) // mem_local == pop
+    fitness_all = jnp.where(slots, jnp.tile(fitness_part, pop_count), 0.0)
+    for rule in (
+        lambda z, y, x, c: (z, y, x, 1 - c),
+        lambda z, y, x, c: (z, y, 1 - x, c),
+        lambda z, y, x, c: (z, 1 - y, x, c),
+        lambda z, y, x, c: (z ^ 1, y, x, c),
+        lambda z, y, x, c: (3 - z, y, x, c),
+    ):
+        fitness_all = fitness_all + send(fitness_all, rule)
+    centered = fitness_all - jnp.mean(fitness_all)
+    scaled = (jnp.repeat(centered, rank)[:, None] * outer_rows.astype(jnp.float32)).astype(jnp.bfloat16)
+    delta = lax.dot_general(
+        scaled, inner_cols, (((0,), (0,)), ((), ())), preferred_element_type=jnp.float32
+    )
+    updated = (
+        weight.astype(jnp.float32) + step_scale / math.sqrt(members_all * rank) * delta
+    ).astype(jnp.bfloat16)
+    return (out, updated)
+
+
 def solution(mesh):
     in_specs = (
         P("pop", "tp"),
@@ -65,4 +300,6 @@
         P("pop", None, "tp"),
     )
     out_specs = (P("pop", "tp"), P("pop", "tp"))
-    return jax.shard_map(local, mesh=mesh, in_specs=in_specs, out_specs=out_specs, check_vma=False)
+    split = mesh.shape["pop"] == 2 * LINE and mesh.shape["tp"] == 4
+    body = local if split else plain
+    return jax.shard_map(body, mesh=mesh, in_specs=in_specs, out_specs=out_specs, check_vma=False)

time: 357 us -> 283 us (0.79)
  starting transfers between devices: 3.46 us -> 82.7 us
  waiting for transfers between devices: 188 us -> 114 us
  blocking collectives: 70.2 us -> 0 us
  local copies, waits for them, and re-layouts: 39.7 us -> 20.9 us
  between operations: 15.4 us -> 1.98 us
  matrix products: 32 us -> 43.1 us
  Pallas kernels: 0 us -> 6.26 us
  other arithmetic: 7.78 us -> 12.4 us
    all_gather x1 -> x0, waiting for transfers between devices: 187 us -> none  [local(): lax.all_gather(weight, 'pop', axis=0, tiled=True)]
    ppermute x0 -> x49, waiting for transfers between devices: none -> 114 us  [send(): return lax.ppermute(array, AXES, pairs)]
    ppermute x0 -> x49, starting transfers between devices: none -> 74.9 us  [send(): return lax.ppermute(array, AXES, pairs)]
    all_gather x1 -> x0, blocking collectives: 31.6 us -> none  [local(): inner_cols = lax.all_gather(factor_in, 'pop', axis=0, tiled=True)]
    unnamed x1 -> x0, blocking collectives: 21.2 us -> none
    psum x2 -> x0, blocking collectives: 17.4 us -> none  [the longest x1 11.8 us: local(): codes_sum = lax.psum(codes_part, 'tp')]
    unnamed x14 -> x60, local copies, waits for them, and re-layouts: 31.3 us -> 15.8 us
    dot_general x4 -> x27, matrix products: 32 us -> 43.1 us  [the longest x24 31.6 us: contract(): lax.dot_general(left, right, (((1,), (1,)), ((), ())), preferred_element_...]
  transfers between devices with their start and end apart: 3 -> 50, of which waited for: 1 -> 16; matrix products, arithmetic and copies ran while one was open for 13% -> 20% of each run, Pallas kernels for 0% -> 0%
where the time goes in v1:
time: 283 us; the launch traced here: 281 us
  waiting for transfers between devices  114 us (40%)
  starting transfers between devices  82.7 us (29%)
  matrix products  43.1 us (15%)
  local copies, waits for them, and re-layouts  20.9 us (7%)
  other arithmetic  12.4 us (4%)
  Pallas kernels  6.26 us (2%)
    ppermute x49, waiting for transfers between devices, send(): return lax.ppermute(array, AXES, pairs)  114 us
    ppermute x49, starting transfers between devices, send(): return lax.ppermute(array, AXES, pairs)  74.9 us
    dot_general x24, matrix products, contract(): lax.dot_general(left, right, (((1,), (1,)), ((), ())), preferred_element_...  31.6 us
    unnamed x60, local copies, waits for them, and re-layouts  15.8 us
    all_to_all x1, starting transfers between devices, split_step(): lax.all_to_all(payload, 'pop', split_axis=0, concat_axis=0, tiled=True)  7.8 us
    pallas_call x1, Pallas kernels, finish(): pl.pallas_call(lambda flags, *refs: finish_body(count, flags, *refs), gri...  6.26 us
  transfers between devices with their start and end apart: 50, of which 16 were waited for; matrix products, arithmetic and copies ran while one was open for 20% of the time, Pallas kernels for 0%

profile of v1, /device:TPU:0, one launch (start us, length us, event | category | flops | bytes accessed | tf_op | source)
XLA Modules:
  0.0 281.2 jit_solution(5833810772516974362)
XLA Ops:
  0.6 3.1 %collective-permute-start.18 = (bf16[640,1280]{1,0:T(8,128)(2,1)}, bf16[640,1280]{1,0:T(8,128)(2,1)S(1)}, u32[]{:S(2)}, u32[]{:S(2)}) collective-permute-start(bf16[640,1280]{1,0:T(8,128)(2,1)} %param.7), channel_id=1, source_target_pairs={{0,8},{1,9},{2,10},{3,11},{4,12},{5,13},{6,14},{7,15},{8,0},{9,1},... | collective-permute-start | bytes 4915208 | tf_op jit(solution)/shard_map/ppermute | solution.py:78
  6.4 1.5 collective-permute-start.6
  9.3 2.5 fusion.19
  11.9 2.2 collective-permute-start.2
  15.2 1.6 collective-permute-start.4
  17.6 7.8 %all-to-all-start = ((bf16[8,16,1920]{2,1,0:T(8,128)(2,1)}), bf16[8,16,1920]{2,1,0:T(8,128)(2,1)}, u32[]{:S(2)}, u32[]{:S(2)}) async-start(bf16[8,16,1920]{2,1,0:T(8,128)(2,1)} %pad_maximum_fusion), calls=%async_computation | async-start | bytes 983040 | tf_op jit(solution)/shard_map/all_to_all | solution.py:227
  28.2 5.5 %convolution_multiply_fusion = f32[4,256,1280]{2,1,0:T(8,128)} fusion(f32[4,4,256]{2,1,0:T(4,128)S(1)} %reshape.26, bf16[4,4,5120]{2,1,0:T(4,128)(2,1)} %param.8, s32[]{:T(128)S(6)} %select_n.152), kind=kOutput, calls=%fused_computation | convolution fusion | flops 64225280 | bytes 5300228 | tf_op jit(solution)/shard_map/mrk,mrc->mkc/dot_general | solution.py:237
  33.7 21.0 %collective-permute-done.15 = bf16[128,1280]{1,0:T(8,128)(2,1)S(1)} collective-permute-done((bf16[128,1280]{1,0:T(8,128)(2,1)}, bf16[128,1280]{1,0:T(8,128)(2,1)S(1)}, u32[]{:S(2)}, u32[]{:S(2)}) %collective-permute-start.15) | collective-permute-done | bytes 327712 | tf_op jit(solution)/shard_map/ppermute | solution.py:78
  56.8 2.3 collective-permute-start.1
  61.6 12.8 %collective-permute-done.7 = bf16[256,1280]{1,0:T(8,128)(2,1)S(1)} collective-permute-done((bf16[256,1280]{1,0:T(8,128)(2,1)}, bf16[256,1280]{1,0:T(8,128)(2,1)S(1)}, u32[]{:S(2)}, u32[]{:S(2)}) %collective-permute-start.7) | collective-permute-done | bytes 655392 | tf_op jit(solution)/shard_map/ppermute | solution.py:78
  76.1 10.7 %collective-permute-done.11 = bf16[256,1280]{1,0:T(8,128)(2,1)S(1)} collective-permute-done((bf16[256,1280]{1,0:T(8,128)(2,1)}, bf16[256,1280]{1,0:T(8,128)(2,1)S(1)}, u32[]{:S(2)}, u32[]{:S(2)}) %collective-permute-start.11) | collective-permute-done | bytes 655392 | tf_op jit(solution)/shard_map/ppermute | solution.py:78
  88.9 9.8 %collective-permute-done.29 = bf16[128,1280]{1,0:T(8,128)(2,1)S(1)} collective-permute-done((bf16[128,1280]{1,0:T(8,128)(2,1)S(1)}, bf16[128,1280]{1,0:T(8,128)(2,1)S(1)}, u32[]{:S(2)}, u32[]{:S(2)}) %collective-permute-start.29) | collective-permute-done | bytes 327712 | tf_op jit(solution)/shard_map/ppermute | solution.py:78
  100.0 2.0 broadcast_select_fusion
  102.1 1.5 collective-permute-start.24
  103.7 1.8 broadcast_select_fusion.1
  105.4 2.1 fusion.25
  108.4 2.0 fusion.6
  111.3 2.0 fusion.4
  115.2 2.0 fusion.20
  117.2 2.0 multiply_convert_fusion.3
  122.1 2.0 fusion.21
  124.1 2.0 multiply_convert_fusion.2
  126.1 1.9 fusion.9
  130.3 1.8 fusion.22
  132.1 1.8 multiply_convert_fusion.5
  137.3 11.5 %collective-permute-done.17 = bf16[1024,128]{1,0:T(8,128)(2,1)S(1)} collective-permute-done((bf16[1024,128]{1,0:T(8,128)(2,1)S(1)}, bf16[1024,128]{1,0:T(8,128)(2,1)S(1)}, u32[]{:S(2)}, u32[]{:S(2)}) %collective-permute-start.17) | collective-permute-done | bytes 262176 | tf_op jit(solution)/shard_map/ppermute | solution.py:78
  150.3 2.4 collective-permute-done.21
  152.7 13.2 %collective-permute-done.25 = bf16[256,1280]{1,0:T(8,128)(2,1)S(1)} collective-permute-done((bf16[256,1280]{1,0:T(8,128)(2,1)}, bf16[256,1280]{1,0:T(8,128)(2,1)S(1)}, u32[]{:S(2)}, u32[]{:S(2)}) %collective-permute-start.25) | collective-permute-done | bytes 655392 | tf_op jit(solution)/shard_map/ppermute | solution.py:78
  167.1 1.5 collective-permute-start.38
  172.1 1.6 collective-permute-start.31
  177.8 2.2 collective-permute-done.31
  182.4 2.5 collective-permute-start.33
  184.8 6.5 %collective-permute-done.23 = bf16[1024,256]{1,0:T(8,128)(2,1)S(1)} collective-permute-done((bf16[1024,256]{1,0:T(8,128)(2,1)S(1)}, bf16[1024,256]{1,0:T(8,128)(2,1)S(1)}, u32[]{:S(2)}, u32[]{:S(2)}) %collective-permute-start.23) | collective-permute-done | bytes 524320 | tf_op jit(solution)/shard_map/ppermute | solution.py:78
  193.6 8.9 %collective-permute-done.27 = bf16[1024,256]{1,0:T(8,128)(2,1)S(1)} collective-permute-done((bf16[1024,256]{1,0:T(8,128)(2,1)S(1)}, bf16[1024,256]{1,0:T(8,128)(2,1)S(1)}, u32[]{:S(2)}, u32[]{:S(2)}) %collective-permute-start.27) | collective-permute-done | bytes 524320 | tf_op jit(solution)/shard_map/ppermute | solution.py:78
  204.8 5.4 %collective-permute-done.40.refs_14_ = bf16[1024,128]{1,0:T(8,128)(2,1)S(1)} collective-permute-done((bf16[1024,128]{1,0:T(8,128)(2,1)S(1)}, bf16[1024,128]{1,0:T(8,128)(2,1)S(1)}, u32[]{:S(2)}, u32[]{:S(2)}) %collective-permute-start.40) | collective-permute-done | bytes 262176 | tf_op jit(solution)/shard_map/ppermute | solution.py:78
  215.3 2.6 collective-permute-start.36
  222.5 2.5 copy-done
  233.0 6.3 %shard_map.68 = (bf16[1024,1280]{1,0:T(8,128)(2,1)}, f32[4,8,128]{2,1,0:T(8,128)S(1)}) custom-call(s32[3]{0:T(128)S(1)} %pad_add_fusion.flags, bf16[1024,256]{1,0:T(8,128)(2,1)S(1)} %add_convert_fusion.3.refs_0_, bf16[1024,256]{1,0:T(8,128)(2,1)S(1)} %copy-done.3, bf16[1024,128]{1,0:T(8,128)(2,1)S(1)} %add_convert_fusion.5.refs_2_, ...), custom_call_target="tpu_custom_call" | custom-call | flops 5242880 | bytes 15728640 | tf_op jit(solution)/shard_map/pallas_call | solution.py:158
  239.5 11.0 %collective-permute-start.44 = (f32[32]{0:T(128)S(1)}, f32[32]{0:T(128)S(1)}, u32[]{:S(2)}, u32[]{:S(2)}) collective-permute-start(f32[32]{0:T(128)S(1)} %compare_select_fusion), channel_id=1, source_target_pairs={{0,1},{1,0},{2,3},{3,2},{4,5},{5,4},{6,7},{7,6},{8,9},{9,8},{10,11... | collective-permute-start | bytes 392 | tf_op jit(solution)/shard_map/ppermute | solution.py:78
  251.3 1.5 collective-permute-start.45
  252.8 2.1 collective-permute-done.45
  254.9 1.7 collective-permute-start.46
  256.6 1.8 collective-permute-done.46
  258.5 10.9 %collective-permute-start.47 = (f32[32]{0:T(128)S(1)}, f32[32]{0:T(128)S(1)}, u32[]{:S(2)}, u32[]{:S(2)}) collective-permute-start(f32[32]{0:T(128)S(1)} %add.121), channel_id=1, source_target_pairs={{0,8},{1,9},{2,10},{3,11},{4,12},{5,13},{6,14},{7,15},{8,0},{9,1},... | collective-permute-start | bytes 392 | tf_op jit(solution)/shard_map/ppermute | solution.py:78
  269.4 1.5 collective-permute-done.47
  270.9 2.1 collective-permute-start.48
  273.0 3.3 %collective-permute-done.48 = f32[32]{0:T(128)S(1)} collective-permute-done((f32[32]{0:T(128)S(1)}, f32[32]{0:T(128)S(1)}, u32[]{:S(2)}, u32[]{:S(2)}) %collective-permute-start.48) | collective-permute-done | bytes 160 | tf_op jit(solution)/shard_map/ppermute | solution.py:78
  277.7 3.5 %fusion.1 = bf16[640,1280]{1,0:T(8,128)(2,1)} fusion(bf16[640,1280]{1,0:T(8,128)(2,1)} %param.7, bf16[128,1920]{1,0:T(8,128)(2,1)} %bitcast.6, f32[128]{0:T(128)S(1)} %mul.76), kind=kOutput, calls=%fused_computation.3 | convolution fusion | flops 213237760 | bytes 3768832 | tf_op jit(solution)/shard_map/dot_general | solution.py:285
  (181 shorter events, 67.3 us)
Async XLA Ops:
  0.6 58.5 %collective-permute-start.18 = (bf16[640,1280]{1,0:T(8,128)(2,1)}, bf16[640,1280]{1,0:T(8,128)(2,1)S(1)}, u32[]{:S(2)}, u32[]{:S(2)}) collective-permute-start(bf16[640,1280]{1,0:T(8,128)(2,1)} %param.7), channel_id=1, source_target_pairs={{0,8},{1,9},{2,10},{3,11},{4,12},{5,13},{6,14},{7,15},{8,0},{9,1},... | collective-permute-start | bytes 4915208 | tf_op jit(solution)/shard_map/ppermute | solution.py:78
  6.4 27.3 %collective-permute-start.6 = (bf16[256,1280]{1,0:T(8,128)(2,1)S(1)}, bf16[256,1280]{1,0:T(8,128)(2,1)}, u32[]{:S(2)}, u32[]{:S(2)}) collective-permute-start(bf16[256,1280]{1,0:T(8,128)(2,1)S(1)} %get-tuple-element.15), channel_id=1, source_target_pairs={{8,16},{9,17},{10,18},{11,19},{12,20},{13,21},{14,22},{15,23},{16,... | collective-permute-start | bytes 1966088 | tf_op jit(solution)/shard_map/ppermute | solution.py:78
  7.9 19.0 %collective-permute-start.14 = (bf16[128,1280]{1,0:T(8,128)(2,1)S(1)}, bf16[128,1280]{1,0:T(8,128)(2,1)}, u32[]{:S(2)}, u32[]{:S(2)}) collective-permute-start(bf16[128,1280]{1,0:T(8,128)(2,1)S(1)} %slice.44), channel_id=1, source_target_pairs={{8,16},{9,17},{10,18},{11,19},{12,20},{13,21},{14,22},{15,23},{16,... | collective-permute-start | bytes 983048 | tf_op jit(solution)/shard_map/ppermute | solution.py:78
  11.9 87.6 %collective-permute-start.2 = (bf16[1024,1280]{1,0:T(8,128)(2,1)}, bf16[1024,1280]{1,0:T(8,128)(2,1)}, u32[]{:S(2)}, u32[]{:S(2)}) collective-permute-start(bf16[1024,1280]{1,0:T(8,128)(2,1)} %param.5), channel_id=1, source_target_pairs={{1,5},{3,7},{5,1},{7,3},{9,13},{11,15},{13,9},{15,11},{17,21},{19,... | collective-permute-start | bytes 7864328 | tf_op jit(solution)/shard_map/ppermute | solution.py:78
  15.2 10.2 %collective-permute-start.4 = (f32[16,256]{1,0:T(8,128)S(1)}, f32[16,256]{1,0:T(8,128)S(1)}, u32[]{:S(2)}, u32[]{:S(2)}) collective-permute-start(f32[16,256]{1,0:T(8,128)S(1)} %add.98), channel_id=1, source_target_pairs={{0,2},{1,3},{2,0},{3,1},{4,6},{5,7},{6,4},{7,5},{8,10},{9,11},{10,... | collective-permute-start | bytes 49160 | tf_op jit(solution)/shard_map/ppermute | solution.py:78
  17.6 87.8 %all-to-all-start = ((bf16[8,16,1920]{2,1,0:T(8,128)(2,1)}), bf16[8,16,1920]{2,1,0:T(8,128)(2,1)}, u32[]{:S(2)}, u32[]{:S(2)}) async-start(bf16[8,16,1920]{2,1,0:T(8,128)(2,1)} %pad_maximum_fusion), calls=%async_computation | async-start | bytes 983040 | tf_op jit(solution)/shard_map/all_to_all | solution.py:227
  25.4 31.4 %collective-permute-start.10 = (bf16[256,1280]{1,0:T(8,128)(2,1)S(1)}, bf16[256,1280]{1,0:T(8,128)(2,1)}, u32[]{:S(2)}, u32[]{:S(2)}) collective-permute-start(bf16[256,1280]{1,0:T(8,128)(2,1)S(1)} %get-tuple-element.17), channel_id=1, source_target_pairs={{8,16},{9,17},{10,18},{11,19},{12,20},{13,21},{14,22},{15,23},{16,... | collective-permute-start | bytes 1966088 | tf_op jit(solution)/shard_map/ppermute | solution.py:78
  26.9 27.8 %collective-permute-start.15 = (bf16[128,1280]{1,0:T(8,128)(2,1)}, bf16[128,1280]{1,0:T(8,128)(2,1)S(1)}, u32[]{:S(2)}, u32[]{:S(2)}) collective-permute-start(bf16[128,1280]{1,0:T(8,128)(2,1)} %collective-permute-done.14), channel_id=1, source_target_pairs={{8,0},{9,1},{10,2},{11,3},{12,4},{13,5},{14,6},{15,7},{16,24},{17,... | collective-permute-start | bytes 983048 | tf_op jit(solution)/shard_map/ppermute | solution.py:78
  33.7 68.3 %collective-permute-start = (bf16[1024,1280]{1,0:T(8,128)(2,1)}, bf16[1024,1280]{1,0:T(8,128)(2,1)S(1)}, u32[]{:S(2)}, u32[]{:S(2)}) collective-permute-start(bf16[1024,1280]{1,0:T(8,128)(2,1)} %param.5), channel_id=1, source_target_pairs={{0,1},{1,0},{2,3},{3,2},{4,5},{5,4},{6,7},{7,6},{8,9},{9,8},{10,11... | collective-permute-start | bytes 7864328 | tf_op jit(solution)/shard_map/ppermute | solution.py:78
  54.7 19.7 %collective-permute-start.7 = (bf16[256,1280]{1,0:T(8,128)(2,1)}, bf16[256,1280]{1,0:T(8,128)(2,1)S(1)}, u32[]{:S(2)}, u32[]{:S(2)}) collective-permute-start(bf16[256,1280]{1,0:T(8,128)(2,1)} %collective-permute-done.6), channel_id=1, source_target_pairs={{8,0},{9,1},{10,2},{11,3},{12,4},{13,5},{14,6},{15,7},{16,24},{17,... | collective-permute-start | bytes 1966088 | tf_op jit(solution)/shard_map/ppermute | solution.py:78
  56.8 45.4 %collective-permute-start.1 = (bf16[1024,1280]{1,0:T(8,128)(2,1)}, bf16[1024,1280]{1,0:T(8,128)(2,1)S(1)}, u32[]{:S(2)}, u32[]{:S(2)}) collective-permute-start(bf16[1024,1280]{1,0:T(8,128)(2,1)} %param.5), channel_id=1, source_target_pairs={{0,5},{2,7},{4,1},{6,3},{8,13},{10,15},{12,9},{14,11},{16,21},{18,... | collective-permute-start | bytes 7864328 | tf_op jit(solution)/shard_map/ppermute | solution.py:78
  59.1 27.6 %collective-permute-start.11 = (bf16[256,1280]{1,0:T(8,128)(2,1)}, bf16[256,1280]{1,0:T(8,128)(2,1)S(1)}, u32[]{:S(2)}, u32[]{:S(2)}) collective-permute-start(bf16[256,1280]{1,0:T(8,128)(2,1)} %collective-permute-done.10), channel_id=1, source_target_pairs={{8,0},{9,1},{10,2},{11,3},{12,4},{13,5},{14,6},{15,7},{16,24},{17,... | collective-permute-start | bytes 1966088 | tf_op jit(solution)/shard_map/ppermute | solution.py:78
  74.4 12.3 %collective-permute-start.28 = (bf16[128,1280]{1,0:T(8,128)(2,1)S(1)}, bf16[128,1280]{1,0:T(8,128)(2,1)S(1)}, u32[]{:S(2)}, u32[]{:S(2)}) collective-permute-start(bf16[128,1280]{1,0:T(8,128)(2,1)S(1)} %slice.61), channel_id=1, source_target_pairs={{8,16},{9,17},{10,18},{11,19},{12,20},{13,21},{14,22},{15,23},{16,... | collective-permute-start | bytes 983048 | tf_op jit(solution)/shard_map/ppermute | solution.py:78
  86.7 20.9 %collective-permute-start.5 = (bf16[640,1280]{1,0:T(8,128)(2,1)}, bf16[640,1280]{1,0:T(8,128)(2,1)}, u32[]{:S(2)}, u32[]{:S(2)}) collective-permute-start(bf16[640,1280]{1,0:T(8,128)(2,1)} %param.7), channel_id=1, source_target_pairs={{0,1},{1,0},{2,3},{3,2},{4,5},{5,4},{6,7},{7,6},{8,9},{9,8},{10,11... | collective-permute-start | bytes 4915208 | tf_op jit(solution)/shard_map/ppermute | solution.py:78
  86.7 12.0 %collective-permute-start.29 = (bf16[128,1280]{1,0:T(8,128)(2,1)S(1)}, bf16[128,1280]{1,0:T(8,128)(2,1)S(1)}, u32[]{:S(2)}, u32[]{:S(2)}) collective-permute-start(bf16[128,1280]{1,0:T(8,128)(2,1)S(1)} %collective-permute-done.28), channel_id=1, source_target_pairs={{8,0},{9,1},{10,2},{11,3},{12,4},{13,5},{14,6},{15,7},{16,24},{17,... | collective-permute-start | bytes 983048 | tf_op jit(solution)/shard_map/ppermute | solution.py:78
  98.7 30.1 %collective-permute-start.16 = (bf16[128,1280]{1,0:T(8,128)(2,1)}, bf16[128,1280]{1,0:T(8,128)(2,1)}, u32[]{:S(2)}, u32[]{:S(2)}) collective-permute-start(bf16[128,1280]{1,0:T(8,128)(2,1)} %broadcast_select_fusion.7), channel_id=1, source_target_pairs={{0,1},{1,0},{2,3},{3,2},{4,5},{5,4},{6,7},{7,6},{8,9},{9,8},{10,11... | collective-permute-start | bytes 983048 | tf_op jit(solution)/shard_map/ppermute | solution.py:78
  99.5 14.7 %collective-permute-start.8 = (bf16[256,1280]{1,0:T(8,128)(2,1)}, bf16[256,1280]{1,0:T(8,128)(2,1)}, u32[]{:S(2)}, u32[]{:S(2)}) collective-permute-start(bf16[256,1280]{1,0:T(8,128)(2,1)} %broadcast_select_fusion.5), channel_id=1, source_target_pairs={{0,1},{1,0},{2,3},{3,2},{4,5},{5,4},{6,7},{7,6},{8,9},{9,8},{10,11... | collective-permute-start | bytes 1966088 | tf_op jit(solution)/shard_map/ppermute | solution.py:78
  102.1 17.2 %collective-permute-start.12 = (bf16[256,1280]{1,0:T(8,128)(2,1)}, bf16[256,1280]{1,0:T(8,128)(2,1)}, u32[]{:S(2)}, u32[]{:S(2)}) collective-permute-start(bf16[256,1280]{1,0:T(8,128)(2,1)} %broadcast_select_fusion.4), channel_id=1, source_target_pairs={{0,1},{1,0},{2,3},{3,2},{4,5},{5,4},{6,7},{7,6},{8,9},{9,8},{10,11... | collective-permute-start | bytes 1966088 | tf_op jit(solution)/shard_map/ppermute | solution.py:78
  102.1 18.5 %collective-permute-start.24 = (bf16[256,1280]{1,0:T(8,128)(2,1)}, bf16[256,1280]{1,0:T(8,128)(2,1)}, u32[]{:S(2)}, u32[]{:S(2)}) collective-permute-start(bf16[256,1280]{1,0:T(8,128)(2,1)} %get-tuple-element.20), channel_id=1, source_target_pairs={{8,16},{9,17},{10,18},{11,19},{12,20},{13,21},{14,22},{15,23},{16,... | collective-permute-start | bytes 1966088 | tf_op jit(solution)/shard_map/ppermute | solution.py:78
  107.6 11.7 %collective-permute-start.20 = (bf16[256,1280]{1,0:T(8,128)(2,1)S(1)}, bf16[256,1280]{1,0:T(8,128)(2,1)S(1)}, u32[]{:S(2)}, u32[]{:S(2)}) collective-permute-start(bf16[256,1280]{1,0:T(8,128)(2,1)S(1)} %copy-done.28), channel_id=1, source_target_pairs={{8,16},{9,17},{10,18},{11,19},{12,20},{13,21},{14,22},{15,23},{16,... | collective-permute-start | bytes 1966088 | tf_op jit(solution)/shard_map/ppermute | solution.py:78
  114.7 52.4 %collective-permute-start.19 = (bf16[640,1280]{1,0:T(8,128)(2,1)S(1)}, bf16[640,1280]{1,0:T(8,128)(2,1)S(1)}, u32[]{:S(2)}, u32[]{:S(2)}) collective-permute-start(bf16[640,1280]{1,0:T(8,128)(2,1)S(1)} %copy-done.22), channel_id=1, source_target_pairs={{0,1},{1,0},{2,3},{3,2},{4,5},{5,4},{6,7},{7,6},{8,9},{9,8},{10,11... | collective-permute-start | bytes 4915208 | tf_op jit(solution)/shard_map/ppermute | solution.py:78
  119.2 16.5 %collective-permute-start.30 = (bf16[128,1280]{1,0:T(8,128)(2,1)S(1)}, bf16[128,1280]{1,0:T(8,128)(2,1)S(1)}, u32[]{:S(2)}, u32[]{:S(2)}) collective-permute-start(bf16[128,1280]{1,0:T(8,128)(2,1)S(1)} %copy-done.23), channel_id=1, source_target_pairs={{0,1},{1,0},{2,3},{3,2},{4,5},{5,4},{6,7},{7,6},{8,9},{9,8},{10,11... | collective-permute-start | bytes 983048 | tf_op jit(solution)/shard_map/ppermute | solution.py:78
  119.3 33.3 %collective-permute-start.21 = (bf16[256,1280]{1,0:T(8,128)(2,1)S(1)}, bf16[256,1280]{1,0:T(8,128)(2,1)S(1)}, u32[]{:S(2)}, u32[]{:S(2)}) collective-permute-start(bf16[256,1280]{1,0:T(8,128)(2,1)S(1)} %collective-permute-done.20), channel_id=1, source_target_pairs={{8,0},{9,1},{10,2},{11,3},{12,4},{13,5},{14,6},{15,7},{16,24},{17,... | collective-permute-start | bytes 1966088 | tf_op jit(solution)/shard_map/ppermute | solution.py:78
  120.6 45.3 %collective-permute-start.25 = (bf16[256,1280]{1,0:T(8,128)(2,1)}, bf16[256,1280]{1,0:T(8,128)(2,1)S(1)}, u32[]{:S(2)}, u32[]{:S(2)}) collective-permute-start(bf16[256,1280]{1,0:T(8,128)(2,1)} %collective-permute-done.24), channel_id=1, source_target_pairs={{8,0},{9,1},{10,2},{11,3},{12,4},{13,5},{14,6},{15,7},{16,24},{17,... | collective-permute-start | bytes 1966088 | tf_op jit(solution)/shard_map/ppermute | solution.py:78
  128.8 37.2 %collective-permute-start.9 = (bf16[1024,256]{1,0:T(8,128)(2,1)S(1)}, bf16[1024,256]{1,0:T(8,128)(2,1)S(1)}, u32[]{:S(2)}, u32[]{:S(2)}) collective-permute-start(bf16[1024,256]{1,0:T(8,128)(2,1)S(1)} %get-tuple-element.32), channel_id=1, source_target_pairs={{0,2},{1,3},{2,0},{3,1},{4,6},{5,7},{6,4},{7,5},{8,10},{9,11},{10,... | collective-permute-start | bytes 1572872 | tf_op jit(solution)/shard_map/ppermute | solution.py:78
  135.8 13.1 %collective-permute-start.17 = (bf16[1024,128]{1,0:T(8,128)(2,1)S(1)}, bf16[1024,128]{1,0:T(8,128)(2,1)S(1)}, u32[]{:S(2)}, u32[]{:S(2)}) collective-permute-start(bf16[1024,128]{1,0:T(8,128)(2,1)S(1)} %get-tuple-element.36), channel_id=1, source_target_pairs={{0,2},{1,3},{2,0},{3,1},{4,6},{5,7},{6,4},{7,5},{8,10},{9,11},{10,... | collective-permute-start | bytes 786440 | tf_op jit(solution)/shard_map/ppermute | solution.py:78
  148.8 18.0 %collective-permute-start.13 = (bf16[1024,256]{1,0:T(8,128)(2,1)S(1)}, bf16[1024,256]{1,0:T(8,128)(2,1)S(1)}, u32[]{:S(2)}, u32[]{:S(2)}) collective-permute-start(bf16[1024,256]{1,0:T(8,128)(2,1)S(1)} %get-tuple-element.34), channel_id=1, source_target_pairs={{0,2},{1,3},{2,0},{3,1},{4,6},{5,7},{6,4},{7,5},{8,10},{9,11},{10,... | collective-permute-start | bytes 1572872 | tf_op jit(solution)/shard_map/ppermute | solution.py:78
  152.7 29.7 %collective-permute-start.34 = (bf16[1024,128]{1,0:T(8,128)(2,1)S(1)}, bf16[1024,128]{1,0:T(8,128)(2,1)S(1)}, u32[]{:S(2)}, u32[]{:S(2)}) collective-permute-start(bf16[1024,128]{1,0:T(8,128)(2,1)S(1)} %add_convert_fusion.5.refs_2_), channel_id=1, source_target_pairs={{0,1},{1,0},{2,3},{3,2},{4,5},{5,4},{6,7},{7,6},{8,9},{9,8},{10,11... | collective-permute-start | bytes 786440 | tf_op jit(solution)/shard_map/ppermute | solution.py:78
  165.9 6.2 %collective-permute-start.22 = (bf16[256,1280]{1,0:T(8,128)(2,1)S(1)}, bf16[256,1280]{1,0:T(8,128)(2,1)S(1)}, u32[]{:S(2)}, u32[]{:S(2)}) collective-permute-start(bf16[256,1280]{1,0:T(8,128)(2,1)S(1)} %broadcast_select_fusion.3), channel_id=1, source_target_pairs={{0,1},{1,0},{2,3},{3,2},{4,5},{5,4},{6,7},{7,6},{8,9},{9,8},{10,11... | collective-permute-start | bytes 1966088 | tf_op jit(solution)/shard_map/ppermute | solution.py:78
  166.0 9.5 %collective-permute-start.26 = (bf16[256,1280]{1,0:T(8,128)(2,1)S(1)}, bf16[256,1280]{1,0:T(8,128)(2,1)S(1)}, u32[]{:S(2)}, u32[]{:S(2)}) collective-permute-start(bf16[256,1280]{1,0:T(8,128)(2,1)S(1)} %broadcast_select_fusion.2), channel_id=1, source_target_pairs={{0,1},{1,0},{2,3},{3,2},{4,5},{5,4},{6,7},{7,6},{8,9},{9,8},{10,11... | collective-permute-start | bytes 1966088 | tf_op jit(solution)/shard_map/ppermute | solution.py:78
  166.8 44.3 %collective-permute-start.32 = (bf16[1024,256]{1,0:T(8,128)(2,1)S(1)}, bf16[1024,256]{1,0:T(8,128)(2,1)S(1)}, u32[]{:S(2)}, u32[]{:S(2)}) collective-permute-start(bf16[1024,256]{1,0:T(8,128)(2,1)S(1)} %add_convert_fusion.3.refs_0_), channel_id=1, source_target_pairs={{0,1},{1,0},{2,3},{3,2},{4,5},{5,4},{6,7},{7,6},{8,9},{9,8},{10,11... | collective-permute-start | bytes 1572872 | tf_op jit(solution)/shard_map/ppermute | solution.py:78
  167.1 47.4 %collective-permute-start.38 = (bf16[1024,256]{1,0:T(8,128)(2,1)S(1)}, bf16[1024,256]{1,0:T(8,128)(2,1)S(1)}, u32[]{:S(2)}, u32[]{:S(2)}) collective-permute-start(bf16[1024,256]{1,0:T(8,128)(2,1)S(1)} %add_convert_fusion.3.refs_0_), channel_id=1, source_target_pairs={{1,4},{3,6},{5,0},{7,2},{9,13},{11,14},{13,9},{15,10},{17,21},{19,... | collective-permute-start | bytes 1572872 | tf_op jit(solution)/shard_map/ppermute | solution.py:78
  172.1 7.9 %collective-permute-start.31 = (bf16[1024,128]{1,0:T(8,128)(2,1)S(1)}, bf16[1024,128]{1,0:T(8,128)(2,1)S(1)}, u32[]{:S(2)}, u32[]{:S(2)}) collective-permute-start(bf16[1024,128]{1,0:T(8,128)(2,1)S(1)} %get-tuple-element.42), channel_id=1, source_target_pairs={{0,2},{1,3},{2,0},{3,1},{4,6},{5,7},{6,4},{7,5},{8,10},{9,11},{10,... | collective-permute-start | bytes 786440 | tf_op jit(solution)/shard_map/ppermute | solution.py:78
  175.5 15.8 %collective-permute-start.23 = (bf16[1024,256]{1,0:T(8,128)(2,1)S(1)}, bf16[1024,256]{1,0:T(8,128)(2,1)S(1)}, u32[]{:S(2)}, u32[]{:S(2)}) collective-permute-start(bf16[1024,256]{1,0:T(8,128)(2,1)S(1)} %get-tuple-element.38), channel_id=1, source_target_pairs={{0,2},{1,3},{2,0},{3,1},{4,6},{5,7},{6,4},{7,5},{8,10},{9,11},{10,... | collective-permute-start | bytes 1572872 | tf_op jit(solution)/shard_map/ppermute | solution.py:78
  180.1 22.5 %collective-permute-start.27 = (bf16[1024,256]{1,0:T(8,128)(2,1)S(1)}, bf16[1024,256]{1,0:T(8,128)(2,1)S(1)}, u32[]{:S(2)}, u32[]{:S(2)}) collective-permute-start(bf16[1024,256]{1,0:T(8,128)(2,1)S(1)} %get-tuple-element.40), channel_id=1, source_target_pairs={{0,2},{1,3},{2,0},{3,1},{4,6},{5,7},{6,4},{7,5},{8,10},{9,11},{10,... | collective-permute-start | bytes 1572872 | tf_op jit(solution)/shard_map/ppermute | solution.py:78
  182.4 29.9 %collective-permute-start.33 = (bf16[1024,256]{1,0:T(8,128)(2,1)S(1)}, bf16[1024,256]{1,0:T(8,128)(2,1)S(1)}, u32[]{:S(2)}, u32[]{:S(2)}) collective-permute-start(bf16[1024,256]{1,0:T(8,128)(2,1)S(1)} %add_convert_fusion.2.refs_1_), channel_id=1, source_target_pairs={{0,1},{1,0},{2,3},{3,2},{4,5},{5,4},{6,7},{7,6},{8,9},{9,8},{10,11... | collective-permute-start | bytes 1572872 | tf_op jit(solution)/shard_map/ppermute | solution.py:78
  191.3 26.7 %collective-permute-start.39 = (bf16[1024,256]{1,0:T(8,128)(2,1)S(1)}, bf16[1024,256]{1,0:T(8,128)(2,1)S(1)}, u32[]{:S(2)}, u32[]{:S(2)}) collective-permute-start(bf16[1024,256]{1,0:T(8,128)(2,1)S(1)} %add_convert_fusion.2.refs_1_), channel_id=1, source_target_pairs={{1,4},{3,6},{5,0},{7,2},{9,13},{11,14},{13,9},{15,10},{17,21},{19,... | collective-permute-start | bytes 1572872 | tf_op jit(solution)/shard_map/ppermute | solution.py:78
  202.5 7.7 %collective-permute-start.40 = (bf16[1024,128]{1,0:T(8,128)(2,1)S(1)}, bf16[1024,128]{1,0:T(8,128)(2,1)S(1)}, u32[]{:S(2)}, u32[]{:S(2)}) collective-permute-start(bf16[1024,128]{1,0:T(8,128)(2,1)S(1)} %add_convert_fusion.5.refs_2_), channel_id=1, source_target_pairs={{1,4},{3,6},{5,0},{7,2},{9,13},{11,14},{13,9},{15,10},{17,21},{19,... | collective-permute-start | bytes 786440 | tf_op jit(solution)/shard_map/ppermute | solution.py:78
  210.9 9.4 %collective-permute-start.37 = (bf16[1024,128]{1,0:T(8,128)(2,1)}, bf16[1024,128]{1,0:T(8,128)(2,1)S(1)}, u32[]{:S(2)}, u32[]{:S(2)}) collective-permute-start(bf16[1024,128]{1,0:T(8,128)(2,1)} %add_convert_fusion.4.refs_5_), channel_id=1, source_target_pairs={{0,1},{1,0},{2,3},{3,2},{4,5},{5,4},{6,7},{7,6},{8,9},{9,8},{10,11... | collective-permute-start | bytes 786440 | tf_op jit(solution)/shard_map/ppermute | solution.py:78
  211.9 10.5 %collective-permute-start.35 = (bf16[1024,256]{1,0:T(8,128)(2,1)}, bf16[1024,256]{1,0:T(8,128)(2,1)}, u32[]{:S(2)}, u32[]{:S(2)}) collective-permute-start(bf16[1024,256]{1,0:T(8,128)(2,1)} %add_convert_fusion.1.refs_3_), channel_id=1, source_target_pairs={{0,1},{1,0},{2,3},{3,2},{4,5},{5,4},{6,7},{7,6},{8,9},{9,8},{10,11... | collective-permute-start | bytes 1572872 | tf_op jit(solution)/shard_map/ppermute | solution.py:78
  213.0 9.4 %collective-permute-start.41 = (bf16[1024,256]{1,0:T(8,128)(2,1)}, bf16[1024,256]{1,0:T(8,128)(2,1)}, u32[]{:S(2)}, u32[]{:S(2)}) collective-permute-start(bf16[1024,256]{1,0:T(8,128)(2,1)} %add_convert_fusion.1.refs_3_), channel_id=1, source_target_pairs={{1,5},{3,7},{5,1},{7,3},{9,12},{11,15},{13,8},{15,11},{17,20},{19,... | collective-permute-start | bytes 1572872 | tf_op jit(solution)/shard_map/ppermute | solution.py:78
  215.3 7.1 %collective-permute-start.36 = (bf16[1024,256]{1,0:T(8,128)(2,1)}, bf16[1024,256]{1,0:T(8,128)(2,1)}, u32[]{:S(2)}, u32[]{:S(2)}) collective-permute-start(bf16[1024,256]{1,0:T(8,128)(2,1)} %add_convert_fusion.refs_4_), channel_id=1, source_target_pairs={{0,1},{1,0},{2,3},{3,2},{4,5},{5,4},{6,7},{7,6},{8,9},{9,8},{10,11... | collective-permute-start | bytes 1572872 | tf_op jit(solution)/shard_map/ppermute | solution.py:78
  218.8 3.6 %collective-permute-start.42 = (bf16[1024,256]{1,0:T(8,128)(2,1)}, bf16[1024,256]{1,0:T(8,128)(2,1)}, u32[]{:S(2)}, u32[]{:S(2)}) collective-permute-start(bf16[1024,256]{1,0:T(8,128)(2,1)} %add_convert_fusion.refs_4_), channel_id=1, source_target_pairs={{1,5},{3,7},{5,1},{7,3},{9,12},{11,15},{13,8},{15,11},{17,20},{19,... | collective-permute-start | bytes 1572872 | tf_op jit(solution)/shard_map/ppermute | solution.py:78
  239.5 11.8 %collective-permute-start.44 = (f32[32]{0:T(128)S(1)}, f32[32]{0:T(128)S(1)}, u32[]{:S(2)}, u32[]{:S(2)}) collective-permute-start(f32[32]{0:T(128)S(1)} %compare_select_fusion), channel_id=1, source_target_pairs={{0,1},{1,0},{2,3},{3,2},{4,5},{5,4},{6,7},{7,6},{8,9},{9,8},{10,11... | collective-permute-start | bytes 392 | tf_op jit(solution)/shard_map/ppermute | solution.py:78
  251.3 3.6 %collective-permute-start.45 = (f32[32]{0:T(128)S(1)}, f32[32]{0:T(128)S(1)}, u32[]{:S(2)}, u32[]{:S(2)}) collective-permute-start(f32[32]{0:T(128)S(1)} %fusion.74), channel_id=1, source_target_pairs={{0,2},{1,3},{2,0},{3,1},{4,6},{5,7},{6,4},{7,5},{8,10},{9,11},{10,... | collective-permute-start | bytes 392 | tf_op jit(solution)/shard_map/ppermute | solution.py:78
  254.9 3.6 %collective-permute-start.46 = (f32[32]{0:T(128)S(1)}, f32[32]{0:T(128)S(1)}, u32[]{:S(2)}, u32[]{:S(2)}) collective-permute-start(f32[32]{0:T(128)S(1)} %add.120), channel_id=1, source_target_pairs={{0,4},{1,5},{2,6},{3,7},{4,0},{5,1},{6,2},{7,3},{8,12},{9,13},{10,... | collective-permute-start | bytes 392 | tf_op jit(solution)/shard_map/ppermute | solution.py:78
  258.5 12.5 %collective-permute-start.47 = (f32[32]{0:T(128)S(1)}, f32[32]{0:T(128)S(1)}, u32[]{:S(2)}, u32[]{:S(2)}) collective-permute-start(f32[32]{0:T(128)S(1)} %add.121), channel_id=1, source_target_pairs={{0,8},{1,9},{2,10},{3,11},{4,12},{5,13},{6,14},{7,15},{8,0},{9,1},... | collective-permute-start | bytes 392 | tf_op jit(solution)/shard_map/ppermute | solution.py:78
  270.9 5.4 %collective-permute-start.48 = (f32[32]{0:T(128)S(1)}, f32[32]{0:T(128)S(1)}, u32[]{:S(2)}, u32[]{:S(2)}) collective-permute-start(f32[32]{0:T(128)S(1)} %add.122), channel_id=1, source_target_pairs={{0,24},{1,25},{2,26},{3,27},{4,28},{5,29},{6,30},{7,31},{8,16},{9,... | collective-permute-start | bytes 392 | tf_op jit(solution)/shard_map/ppermute | solution.py:78
  (32 other events, 198.0 us)

commit v2 on v1

--- a/solution.py
+++ b/solution.py
@@ -14,6 +14,7 @@
 AXES = ("pop", "tp")
 LINE = 4
 LANES = 128
+VMEM_GRANT = 24 * 1024 * 1024
 
 
 def plain(tokens, target, weight, factor_out, factor_in):
@@ -83,87 +84,104 @@
 
 
 def cuts(rows):
-    blocks = rows // LANES
-    wide = max(1, (blocks - 1) // 2)
-    edges = sorted({0, wide * LANES, (blocks - 1) * LANES, blocks * LANES})
-    return tuple(zip(edges[:-1], edges[1:]))
+    narrow = rows // LANES // 2 * LANES
+    return ((0, narrow), (narrow, rows)), ((0, narrow), (narrow, rows - LANES), (rows - LANES, rows))
 
 
 def contract(left, right):
     return lax.dot_general(left, right, (((1,), (1,)), ((), ())), preferred_element_type=jnp.float32)
 
 
-def finish_body(count, flags, *refs):
-    totals, sides, others = (refs[2 * count * g : 2 * count * (g + 1)] for g in range(3))
-    low_ref, want_ref, out_ref, fit_ref = refs[6 * count :]
-    half = pl.program_id(1)
-
-    def emit(group):
-        base = jnp.concatenate([ref[...] for ref in group], axis=1)
-        value = base.astype(jnp.float32) + low_ref[...]
-        out_ref[...] = value.astype(out_ref.dtype)
-        product = value * want_ref[...].astype(jnp.float32)
-        rows, cols = product.shape
-        folded = product.reshape(rows // 8, 8, cols).sum(axis=0)
-        lanes = sum(folded[:, lo : lo + LANES] for lo in range(0, cols, LANES))
-
-        @pl.when(half == 0)
-        def _():
-            fit_ref[0] = lanes
-
-        @pl.when(half == 1)
-        def _():
-            fit_ref[0] += lanes
-
+def choose(flags, half, totals, sides, others, emit):
     for step in range(2):
         here = flags[0] == step
-        part = slice(step * count, (step + 1) * count)
 
         @pl.when(here & (half == 0) & (flags[1] == 0))
         def _():
-            emit(totals[part])
+            emit(step, totals[step])
 
         @pl.when(here & (half == 0) & (flags[1] == 1))
         def _():
-            emit(sides[part])
+            emit(step, sides[step])
 
         @pl.when(here & (half == 1))
         def _():
-            emit(others[part])
-
-
-def finish(flags, totals, sides, others, low_rank, target, members):
-    rows, width = low_rank.shape
-    block = rows // members
-    count = len(totals) // 2
+            emit(step, others[step])
+
+
+def fold(product):
+    rows, cols = product.shape
+    folded = product.reshape(rows // 8, 8, cols).sum(axis=0)
+    return sum(folded[:, lo : lo + LANES] for lo in range(0, cols, LANES))
+
+
+def needed(step, side):
+    if side is None:
+        return lambda flags: flags[0] == step
+    return lambda flags: (flags[0] == step) & (flags[1] == side)
+
+
+def finish_most(flags, totals, sides, others, low_rank, target, members):
+    rows, width = target.shape
+    together = 2 if members % 2 == 0 else 1
+    block, half_width = rows // members * together, width // 2
+    groups = [group for step in range(2) for group in ((0, totals[step]), (1, sides[step]), (None, others[step]))]
+
+    def body(flags, *refs):
+        picked, at = [], 0
+        for _, arrays in groups:
+            picked.append(refs[at : at + len(arrays)])
+            at += len(arrays)
+        low_ref, want_ref, out_ref, fit_ref = refs[at:]
+        half = pl.program_id(1)
+
+        def emit(step, group):
+            parts = [ref[...] for ref in group]
+            have = sum(part.shape[1] for part in parts)
+            if have < half_width:
+                parts.append(jnp.zeros((block, half_width - have), parts[0].dtype))
+            value = jnp.concatenate(parts, axis=1).astype(jnp.float32)
+            value += low_ref[...].astype(jnp.float32)
+            out_ref[...] = value.astype(out_ref.dtype)
+            product = value * want_ref[...].astype(jnp.float32)
+            size = block // together
+            for m in range(together):
+                lanes = fold(product[m * size : (m + 1) * size])
+
+                @pl.when(half == 0)
+                def _():
+                    fit_ref[m] = lanes
+
+                @pl.when(half == 1)
+                def _():
+                    fit_ref[m] += lanes
+
+        choose(flags, half, picked[0::3], picked[1::3], picked[2::3], emit)
 
     def column(m, h, flags):
-        own = flags[2]
-        return (m, jnp.where(h == 0, own, 1 - own))
-
-    def spec(array, want):
-        return pl.BlockSpec(
-            (block, array.shape[1]), lambda m, h, flags: (jnp.where(want(flags), m, 0), 0)
-        )
-
-    specs = []
-    for group, side in ((totals, 0), (sides, 1), (others, None)):
-        for i, array in enumerate(group):
-            step = i // count
-            if side is None:
-                specs.append(spec(array, lambda f, s=step: f[0] == s))
-            else:
-                specs.append(spec(array, lambda f, s=step, d=side: (f[0] == s) & (f[1] == d)))
-    specs += [pl.BlockSpec((block, width // 2), column)] * 2
+        return (m, jnp.where(h == 0, flags[2], 1 - flags[2]))
+
+    specs, operands = [], []
+    for i, (side, arrays) in enumerate(groups):
+        want = needed(i // 3, side)
+        for array in arrays:
+            specs.append(
+                pl.BlockSpec(
+                    (block, array.shape[1]),
+                    lambda m, h, flags, want=want: (jnp.where(want(flags), m, 0), 0),
+                )
+            )
+            operands.append(array)
+    specs += [pl.BlockSpec((block, half_width), column)] * 2
     return pl.pallas_call(
-        lambda flags, *refs: finish_body(count, flags, *refs),
+        body,
         grid_spec=pltpu.PrefetchScalarGridSpec(
             num_scalar_prefetch=1,
-            grid=(members, 2),
+            grid=(members // together, 2),
             in_specs=specs,
             out_specs=[
-                pl.BlockSpec((block, width // 2), column),
-                pl.BlockSpec((1, 8, LANES), lambda m, h, flags: (m, 0, 0)),
+                pl.BlockSpec((block, half_width), column),
+                pl.BlockSpec((together, 8, LANES), lambda m, h, flags: (m, 0, 0)),
             ],
         ),
         out_shape=[
@@ -173,8 +191,73 @@
         cost_estimate=pl.CostEstimate(
             flops=4 * rows * width, bytes_accessed=12 * rows * width, transcendentals=0
         ),
-        compiler_params=pltpu.CompilerParams(vmem_limit_bytes=16 * 1024 * 1024),
-    )(flags, *totals, *sides, *others, low_rank, target)
+        compiler_params=pltpu.CompilerParams(vmem_limit_bytes=VMEM_GRANT),
+    )(flags, *operands, low_rank, target)
+
+
+def finish_last(flags, piece, totals, sides, others, low_rank, target, members, out):
+    lo, hi = piece
+    rows, width = target.shape
+    half_blocks, first = width // 2 // LANES, lo // LANES
+    operands = [array for step in range(2) for array in (totals[step], sides[step], others[step])]
+
+    def body(flags, *refs):
+        low_ref, want_ref, _, out_ref, fit_ref = refs[6:]
+
+        @pl.when((pl.program_id(0) == 0) & (pl.program_id(1) == 0))
+        def _():
+            fit_ref[...] = jnp.zeros_like(fit_ref)
+
+        def emit(step, ref):
+            base = ref[...].astype(jnp.float32)
+            out_ref[...] = (base + low_ref[...].astype(jnp.float32)).astype(out_ref.dtype)
+            if step == 1:
+                product = base * want_ref[...].astype(jnp.float32)
+                size = rows // members
+                for m in range(members):
+                    fit_ref[m] += fold(product[m * size : (m + 1) * size])
+
+        choose(flags, pl.program_id(1), refs[0:6:3], refs[1:6:3], refs[2:6:3], emit)
+
+    def column(j, h, flags):
+        return (0, jnp.where(h == 0, flags[2], 1 - flags[2]) * half_blocks + first + j)
+
+    specs = []
+    for i, array in enumerate(operands):
+        want = needed(i // 3, (0, 1, None)[i % 3])
+        start = (array.shape[1] - (hi - lo)) // LANES
+        specs.append(
+            pl.BlockSpec(
+                (rows, LANES),
+                lambda j, h, flags, want=want, start=start: (0, jnp.where(want(flags), start + j, 0)),
+            )
+        )
+    specs += [
+        pl.BlockSpec((rows, LANES), column),
+        pl.BlockSpec((rows, LANES), column),
+        pl.BlockSpec(memory_space=pl.ANY),
+    ]
+    return pl.pallas_call(
+        body,
+        grid_spec=pltpu.PrefetchScalarGridSpec(
+            num_scalar_prefetch=1,
+            grid=((hi - lo) // LANES, 2),
+            in_specs=specs,
+            out_specs=[
+                pl.BlockSpec((rows, LANES), column),
+                pl.BlockSpec((members, 8, LANES), lambda j, h, flags: (0, 0, 0)),
+            ],
+        ),
+        out_shape=[
+            jax.ShapeDtypeStruct((rows, width), out.dtype),
+            jax.ShapeDtypeStruct((members, 8, LANES), jnp.float32),
+        ],
+        input_output_aliases={9: 0},
+        cost_estimate=pl.CostEstimate(
+            flops=4 * rows * (hi - lo), bytes_accessed=20 * rows * (hi - lo), transcendentals=0
+        ),
+        compiler_params=pltpu.CompilerParams(vmem_limit_bytes=VMEM_GRANT),
+    )(flags, *operands, low_rank, target, out)
 
 
 def local(tokens, target, weight, factor_out, factor_in):
@@ -198,22 +281,23 @@
     bit = jnp.where(near_first, z % 2, z // 2)
     flags = jnp.stack([c ^ bit, c, y]).astype(jnp.int32)
     pieces = cuts(weight_rows)
-    count = len(pieces)
-    sub = lambda array: [array[lo:hi] for lo, hi in pieces]
+    sub = lambda array, step: [array[lo:hi] for lo, hi in pieces[step]]
 
     partner = lambda z, y, x, c: (z, y, x, 1 - c)
 
     mid = lambda z, y, x, c: (3 - z, y, x, c) if z in (1, 2) else None
     end = lambda z, y, x, c: (z ^ 1, y, x, c) if z in (1, 2) else None
     swap = send(weight, lambda z, y, x, c: (z ^ 1, y, x, c))
-    early = [lax.optimization_barrier(sub(weight)), lax.optimization_barrier(sub(swap))]
+    early = [lax.optimization_barrier(sub(weight, 0)), lax.optimization_barrier(sub(swap, 1))]
     early_o = [send(weight, partner), send(swap, partner)]
     rows_a = send(tokens, lambda z, y, x, c: (z, 1 - y, x, 1) if c == 0 else None)
     rows_p = send(tokens, partner)
     rows_b = send(tokens, lambda z, y, x, c: (z, 1 - y, x, 1) if c == 1 else None)
-    at_mid = [[send(early[s][k], mid) for k in range(count)] for s in range(2)]
-    at_end = [[send(at_mid[s][k], end) for k in range(count)] for s in range(2)]
-    rows_a, rows_b = jnp.where(c == 0, rows_p, rows_a), jnp.where(c == 0, tokens, rows_b)
+    at_mid = [[send(w, mid) for w in early[s]] for s in range(2)]
+    at_end = [[send(w, end) for w in at_mid[s]] for s in range(2)]
+    rows = jnp.concatenate(
+        [jnp.where(c == 0, tokens, rows_b), jnp.where(c == 0, rows_p, rows_a)], axis=1
+    )
 
     outer_flat = factor_out.reshape(mem_local * rank, width_out)
     inner_flat = factor_in.reshape(mem_local * rank, shard_width)
@@ -224,9 +308,6 @@
         ],
         axis=2,
     )
-    factors = lax.all_to_all(payload, "pop", split_axis=0, concat_axis=0, tiled=True)
-    factors = factors.reshape(pop_count * mem_local * rank, weight_rows + shard_width)
-
     token_sets = tokens.reshape(mem_local, tok_member, shard_width)
     codes = jnp.einsum("mkc,mrc->mrk", token_sets, factor_in, preferred_element_type=jnp.float32)
     codes = codes.reshape(mem_local * rank, tok_member)
@@ -237,38 +318,54 @@
     low_rank = jnp.einsum(
         "mrk,mrc->mkc", codes, outer_cols, precision=lax.Precision.HIGHEST
     ) * (noise_scale / math.sqrt(rank * width_in))
-    low_rank = low_rank.reshape(tok_rows, out_cols)
-
-    rows_a, rows_b, low_rank, factors = lax.optimization_barrier((rows_a, rows_b, low_rank, factors))
-    outer_rows, inner_cols = factors[:, :weight_rows], factors[:, weight_rows:]
-    early_sum = [[None] * count, [None] * count]
+    low_rank = low_rank.astype(target.dtype).reshape(tok_rows, out_cols)
+
+    rows, low_rank, payload = lax.optimization_barrier((rows, low_rank, payload))
+    factors = lax.all_to_all(payload, "pop", split_axis=0, concat_axis=0, tiled=True)
+    factors = factors.reshape(pop_count * mem_local * rank, weight_rows + shard_width)
+    early_sum = [[None] * len(part) for part in pieces]
     for step in range(2):
-        for k, (lo, hi) in enumerate(pieces):
-            early_sum[step][k] = contract(rows_b, early[step][k]) + contract(
-                rows_a, early_o[step][lo:hi]
-            )
-    totals, sides, others = [], [], []
+        for k, (lo, hi) in enumerate(pieces[step]):
+            block = jnp.concatenate([early[step][k], early_o[step][lo:hi]], axis=1)
+            early_sum[step][k] = contract(rows, block)
+    totals, sides, others = ([], []), ([], []), ([], [])
     for step in range(2):
-        for k in range(count):
+        for k in range(len(pieces[step])):
             last = jnp.where(inner, at_mid[step][k], at_end[step][k])
             last_o = send(last, partner)
-            last_sum = contract(rows_b, last) + contract(rows_a, last_o)
+            last_sum = contract(rows, jnp.concatenate([last, last_o], axis=1))
             far_sum = jnp.where(near_first, last_sum, early_sum[step][k]) * base_factor
             near_sum = jnp.where(near_first, early_sum[step][k], last_sum) * base_factor
             far_sum = far_sum.astype(jnp.bfloat16)
             moved = send(far_sum, lambda z, y, x, c: (z, y, 1 - x, c))
             total = (near_sum + moved.astype(jnp.float32)).astype(jnp.bfloat16)
-            totals.append(total)
-            sides.append(send(total, partner))
-            others.append(
+            totals[step].append(total)
+            sides[step].append(send(total, partner))
+            others[step].append(
                 send(
                     total,
                     lambda z, y, x, c: (z, 1 - y, x, keep_core(z, x, step)) if c == 1 else None,
                 )
             )
 
-    out, fits = finish(flags, totals, sides, others, low_rank, target, mem_local)
-    fitness_part = jnp.sum(fits, axis=(1, 2)) / (tok_member * math.sqrt(width_out))
+    outer_rows, inner_cols = factors[:, :weight_rows], factors[:, weight_rows:]
+    most = lambda arrays: (arrays[0], arrays[1][:-1])
+    out, fits = finish_most(
+        flags, most(totals), most(sides), most(others), low_rank, target, mem_local
+    )
+    tail = lambda arrays: (arrays[0][-1], arrays[1][-1])
+    out, last_fits = finish_last(
+        flags,
+        pieces[1][-1],
+        tail(totals),
+        tail(sides),
+        tail(others),
+        low_rank,
+        target,
+        mem_local,
+        out,
+    )
+    fitness_part = jnp.sum(fits + last_fits, axis=(1, 2)) / (tok_member * math.sqrt(width_out))
     members_all = pop_count * mem_local
     slots = jnp.arange(members_all) // mem_local == pop
     fitness_all = jnp.where(slots, jnp.tile(fitness_part, pop_count), 0.0)

time: 283 us -> 252 us (0.89)
  starting transfers between devices: 82.7 us -> 58.5 us
  matrix products: 43.1 us -> 30.3 us
  waiting for transfers between devices: 114 us -> 119 us
    ppermute x49 -> x43, starting transfers between devices: 74.9 us -> 51.5 us  [send(): return lax.ppermute(array, AXES, pairs)]
    dot_general x24 -> x10, matrix products: 31.6 us -> 21.9 us  [contract(): lax.dot_general(left, right, (((1,), (1,)), ((), ())), preferred_element_...]
    slice x4 -> x8, local copies, waits for them, and re-layouts: 3.76 us -> 9.41 us  [the longest x4 6.07 us: split_step(): sub = lambda array, step: [array[lo:hi] for lo, hi in pieces[step]]]
    ppermute x49 -> x43, waiting for transfers between devices: 114 us -> 119 us  [send(): return lax.ppermute(array, AXES, pairs)]
    unnamed x60 -> x56, local copies, waits for them, and re-layouts: 15.8 us -> 11.1 us
    dot_general x1, matrix products: 5.51 us -> 2.4 us  [split_step(): jnp.einsum('mrk,mrc->mkc', codes, outer_cols, precision=lax.Precision.HIG...]
    pallas_call x1 -> x2, Pallas kernels: 6.26 us -> 8.04 us  [the longest x1 5.06 us: finish_most(): pl.pallas_call(body, grid_spec=pltpu.PrefetchScalarGridSpec(num_scalar_pr...]
  transfers between devices with their start and end apart: 50 -> 44, of which waited for: 16 -> 17; matrix products, arithmetic and copies ran while one was open for 20% -> 19% of each run, Pallas kernels for 0% -> 3%
where the time goes in v2:
time: 252 us; the launch traced here: 251 us
  waiting for transfers between devices  119 us (47%)
  starting transfers between devices  58.5 us (23%)
  matrix products  30.3 us (12%)
  local copies, waits for them, and re-layouts  21 us (8%)
  other arithmetic  12 us (5%)
  Pallas kernels  8.04 us (3%)
    ppermute x43, waiting for transfers between devices, send(): return lax.ppermute(array, AXES, pairs)  119 us
    ppermute x43, starting transfers between devices, send(): return lax.ppermute(array, AXES, pairs)  51.5 us
    dot_general x10, matrix products, contract(): lax.dot_general(left, right, (((1,), (1,)), ((), ())), preferred_element_...  21.9 us
    unnamed x56, local copies, waits for them, and re-layouts  11.1 us
    all_to_all x1, starting transfers between devices, split_step(): lax.all_to_all(payload, 'pop', split_axis=0, concat_axis=0, tiled=True)  6.95 us
    slice x4, local copies, waits for them, and re-layouts, split_step(): sub = lambda array, step: [array[lo:hi] for lo, hi in pieces[step]]  6.07 us
    pallas_call x1, Pallas kernels, finish_most(): pl.pallas_call(body, grid_spec=pltpu.PrefetchScalarGridSpec(num_scalar_pr...  5.06 us
  transfers between devices with their start and end apart: 44, of which 17 were waited for; matrix products, arithmetic and copies ran while one was open for 19% of the time, Pallas kernels for 3%

profile of v2, /device:TPU:0, one launch (start us, length us, event | category | flops | bytes accessed | tf_op | source)
XLA Modules:
  0.0 250.7 jit_solution(18366345669136573743)
XLA Ops:
  0.6 3.1 %collective-permute-start.12 = (bf16[640,1280]{1,0:T(8,128)(2,1)}, bf16[640,1280]{1,0:T(8,128)(2,1)}, u32[]{:S(2)}, u32[]{:S(2)}) collective-permute-start(bf16[640,1280]{1,0:T(8,128)(2,1)} %param.7), channel_id=1, source_target_pairs={{0,8},{1,9},{2,10},{3,11},{4,12},{5,13},{6,14},{7,15},{8,0},{9,1},... | collective-permute-start | bytes 4915208 | tf_op jit(solution)/shard_map/ppermute | solution.py:79
  4.9 2.5 slice.37
  8.2 1.7 collective-permute-start.6
  11.2 2.5 %fusion.60 = f32[4,4,256]{2,1,0:T(4,128)S(1)} fusion(bf16[4,4,1280]{2,1,0:T(4,128)(2,1)S(1)} %copy-done.27, bf16[4,256,1280]{2,1,0:T(8,128)(2,1)} %bitcast.3), kind=kOutput, calls=%fused_computation.91 | convolution fusion | flops 10485760 | bytes 2678784 | tf_op jit(solution)/shard_map/mkc,mrc->mrk/dot_general | solution.py:312
  15.1 1.5 collective-permute-start.4
  16.8 2.0 collective-permute-done.4
  18.9 2.2 collective-permute-start
  21.9 2.4 multiply_convert_fusion
  24.3 16.4 %collective-permute-done.12 = bf16[640,1280]{1,0:T(8,128)(2,1)} collective-permute-done((bf16[640,1280]{1,0:T(8,128)(2,1)}, bf16[640,1280]{1,0:T(8,128)(2,1)}, u32[]{:S(2)}, u32[]{:S(2)}) %collective-permute-start.12) | collective-permute-done | bytes 1638432 | tf_op jit(solution)/shard_map/ppermute | solution.py:79
  41.8 4.1 %collective-permute-start.2 = (bf16[1024,1280]{1,0:T(8,128)(2,1)}, bf16[1024,1280]{1,0:T(8,128)(2,1)S(1)}, u32[]{:S(2)}, u32[]{:S(2)}) collective-permute-start(bf16[1024,1280]{1,0:T(8,128)(2,1)} %param.5), channel_id=1, source_target_pairs={{0,5},{2,7},{4,1},{6,3},{8,13},{10,15},{12,9},{14,11},{16,21},{18,... | collective-permute-start | bytes 7864328 | tf_op jit(solution)/shard_map/ppermute | solution.py:79
  45.9 8.0 %collective-permute-done.21 = bf16[256,1280]{1,0:T(8,128)(2,1)} collective-permute-done((bf16[256,1280]{1,0:T(8,128)(2,1)S(1)}, bf16[256,1280]{1,0:T(8,128)(2,1)}, u32[]{:S(2)}, u32[]{:S(2)}) %collective-permute-start.21) | collective-permute-done | bytes 655392 | tf_op jit(solution)/shard_map/ppermute | solution.py:79
  57.3 2.0 broadcast_select_fusion.5
  60.6 2.0 slice.53
  62.6 16.3 %collective-permute-done.7 = bf16[384,1280]{1,0:T(8,128)(2,1)S(1)} collective-permute-done((bf16[384,1280]{1,0:T(8,128)(2,1)}, bf16[384,1280]{1,0:T(8,128)(2,1)S(1)}, u32[]{:S(2)}, u32[]{:S(2)}) %collective-permute-start.7) | collective-permute-done | bytes 983072 | tf_op jit(solution)/shard_map/ppermute | solution.py:79
  80.4 8.5 %collective-permute-done.15 = bf16[128,1280]{1,0:T(8,128)(2,1)S(1)} collective-permute-done((bf16[128,1280]{1,0:T(8,128)(2,1)S(1)}, bf16[128,1280]{1,0:T(8,128)(2,1)S(1)}, u32[]{:S(2)}, u32[]{:S(2)}) %collective-permute-start.15) | collective-permute-done | bytes 327712 | tf_op jit(solution)/shard_map/ppermute | solution.py:79
  88.8 1.6 collective-permute-start.26
  92.7 2.0 broadcast_select_fusion.1
  97.3 4.2 %fusion.2 = f32[1024,384]{1,0:T(8,128)S(1)} fusion(bf16[1024,2560]{1,0:T(8,128)(2,1)S(1)} %pad_maximum_fusion, bf16[384,1280]{1,0:T(8,128)(2,1)S(1)} %slice.48, bf16[384,1280]{1,0:T(8,128)(2,1)} %slice.37), kind=kOutput, calls=%fused_computation.7 | convolution fusion | flops 2017198080 | bytes 8781824 | tf_op jit(solution)/shard_map/dot_general | solution.py:92
  101.5 1.5 fusion.10
  104.7 2.8 %multiply_convert_fusion.4 = (bf16[1024,256]{1,0:T(8,128)(2,1)S(1)}, f32[1024,256]{1,0:T(8,128)S(1)}) fusion(f32[1024,256]{1,0:T(8,128)S(1)} %fusion.10, pred[]{:T(512)S(6)} %eq.23, bf16[1024,2560]{1,0:T(8,128)(2,1)S(1)} %pad_maximum_fusion, bf16[256,1280]{1,0:T(8,128)(2,1)} %collective-permute-done.22, bf16[256,1280]{1,0:T(8,128)(2,1)} %broadcast_select_fusion.5), kind=kOutput, calls=%fused_computation.46 | convolution fusion | flops 1345585152 | bytes 9175041 | tf_op jit(solution)/shard_map/dot_general | solution.py:92
  107.6 18.4 %collective-permute-done.27 = bf16[256,1280]{1,0:T(8,128)(2,1)} collective-permute-done((bf16[256,1280]{1,0:T(8,128)(2,1)}, bf16[256,1280]{1,0:T(8,128)(2,1)}, u32[]{:S(2)}, u32[]{:S(2)}) %collective-permute-start.27) | collective-permute-done | bytes 655392 | tf_op jit(solution)/shard_map/ppermute | solution.py:79
  126.0 1.5 collective-permute-start.23
  128.6 10.7 %collective-permute-done.31 = bf16[256,1280]{1,0:T(8,128)(2,1)S(1)} collective-permute-done((bf16[256,1280]{1,0:T(8,128)(2,1)}, bf16[256,1280]{1,0:T(8,128)(2,1)S(1)}, u32[]{:S(2)}, u32[]{:S(2)}) %collective-permute-start.31) | collective-permute-done | bytes 655392 | tf_op jit(solution)/shard_map/ppermute | solution.py:79
  140.0 4.1 %multiply_convert_fusion.1 = (bf16[1024,384]{1,0:T(8,128)(2,1)S(1)}, f32[1024,384]{1,0:T(8,128)S(1)}) fusion(f32[1024,384]{1,0:T(8,128)S(1)} %fusion.2, pred[]{:T(512)S(6)} %eq.23, bf16[1024,2560]{1,0:T(8,128)(2,1)S(1)} %pad_maximum_fusion, bf16[384,1280]{1,0:T(8,128)(2,1)} %collective-permute-done.8, bf16[384,1280]{1,0:T(8,128)(2,1)S(1)} %copy-done.15), kind=kOutput, calls=%fused_computation.16 | convolution fusion | flops 2018377728 | bytes 11141121 | tf_op jit(solution)/shard_map/dot_general | solution.py:92
  144.1 1.6 collective-permute-start.9
  145.7 1.5 fusion.34
  147.2 1.5 multiply_convert_fusion.5
  149.8 1.5 fusion.18
  151.3 1.5 fusion.26
  152.9 1.6 multiply_convert_fusion.3
  155.6 1.5 multiply_convert_fusion.2
  158.2 6.4 %collective-permute-done.9 = bf16[1024,384]{1,0:T(8,128)(2,1)S(1)} collective-permute-done((bf16[1024,384]{1,0:T(8,128)(2,1)S(1)}, bf16[1024,384]{1,0:T(8,128)(2,1)S(1)}, u32[]{:S(2)}, u32[]{:S(2)}) %collective-permute-start.9) | collective-permute-done | bytes 786464 | tf_op jit(solution)/shard_map/ppermute | solution.py:79
  165.8 4.4 %collective-permute-done.17 = bf16[1024,128]{1,0:T(8,128)(2,1)S(1)} collective-permute-done((bf16[1024,128]{1,0:T(8,128)(2,1)S(1)}, bf16[1024,128]{1,0:T(8,128)(2,1)S(1)}, u32[]{:S(2)}, u32[]{:S(2)}) %collective-permute-start.17) | collective-permute-done | bytes 262176 | tf_op jit(solution)/shard_map/ppermute | solution.py:79
  171.5 9.9 %collective-permute-done.29 = bf16[1024,256]{1,0:T(8,128)(2,1)S(1)} collective-permute-done((bf16[1024,256]{1,0:T(8,128)(2,1)S(1)}, bf16[1024,256]{1,0:T(8,128)(2,1)S(1)}, u32[]{:S(2)}, u32[]{:S(2)}) %collective-permute-start.29) | collective-permute-done | bytes 524320 | tf_op jit(solution)/shard_map/ppermute | solution.py:79
  183.7 8.0 %collective-permute-done.33 = bf16[1024,256]{1,0:T(8,128)(2,1)S(1)} collective-permute-done((bf16[1024,256]{1,0:T(8,128)(2,1)S(1)}, bf16[1024,256]{1,0:T(8,128)(2,1)S(1)}, u32[]{:S(2)}, u32[]{:S(2)}) %collective-permute-start.33) | collective-permute-done | bytes 524320 | tf_op jit(solution)/shard_map/ppermute | solution.py:79
  195.0 2.2 collective-permute-start.35
  203.3 6.9 %all-to-all-start = ((bf16[8,16,1920]{2,1,0:T(8,128)(2,1)}), bf16[8,16,1920]{2,1,0:T(8,128)(2,1)}, u32[]{:S(2)}, u32[]{:S(2)}) async-start(bf16[8,16,1920]{2,1,0:T(8,128)(2,1)} %pad_maximum_fusion.1), calls=%async_computation | async-start | bytes 983040 | tf_op jit(solution)/shard_map/all_to_all | solution.py:324
  210.3 1.7 copy-done
  218.4 5.1 %shard_map.68 = (bf16[1024,1280]{1,0:T(8,128)(2,1)}, f32[4,8,128]{2,1,0:T(8,128)S(1)}) custom-call(s32[3]{0:T(128)S(1)} %pad_add_fusion.flags, bf16[1024,256]{1,0:T(8,128)(2,1)S(1)} %copy-done.7, bf16[1024,384]{1,0:T(8,128)(2,1)S(1)} %add_convert_fusion.refs_1_.refs_0_, bf16[1024,256]{1,0:T(8,128)(2,1)S(1)} %copy-done.9, bf16[1024,384]{1,0:T(8,128)(2,1)S(1)} %copy-done.3, ...), custom_call_target="tpu_custom_call" | custom-call | flops 5242880 | bytes 15728640 | tf_op jit(solution)/shard_map/pallas_call | solution.py:176
  223.5 3.0 %shard_map.69 = (bf16[1024,1280]{1,0:T(8,128)(2,1)}, f32[4,8,128]{2,1,0:T(8,128)S(1)}) custom-call(s32[3]{0:T(128)S(1)} %pad_add_fusion.flags, bf16[1024,384]{1,0:T(8,128)(2,1)S(1)} %add_convert_fusion.refs_1_.refs_0_, bf16[1024,384]{1,0:T(8,128)(2,1)S(1)} %copy-done.3, bf16[1024,384]{1,0:T(8,128)(2,1)S(1)} %copy-done.5, ...), custom_call_target="tpu_custom_call", output_to_operand_aliasing={{0}: (9, {})} | custom-call | flops 524288 | bytes 2621440 | tf_op jit(solution)/shard_map/pallas_call | solution.py:240
  226.7 2.1 collective-permute-start.38
  231.1 2.1 collective-permute-done.39
  233.2 1.7 collective-permute-start.40
  234.9 1.8 collective-permute-done.40
  238.2 2.2 collective-permute-done.41
  240.4 3.2 %collective-permute-start.42 = (f32[32]{0:T(128)S(1)}, f32[32]{0:T(128)S(1)}, u32[]{:S(2)}, u32[]{:S(2)}) collective-permute-start(f32[32]{0:T(128)S(1)} %add.74), channel_id=1, source_target_pairs={{0,24},{1,25},{2,26},{3,27},{4,28},{5,29},{6,30},{7,31},{8,16},{9,... | collective-permute-start | bytes 392 | tf_op jit(solution)/shard_map/ppermute | solution.py:79
  243.5 2.2 collective-permute-done.42
  247.2 3.5 %fusion.1 = bf16[640,1280]{1,0:T(8,128)(2,1)} fusion(bf16[640,1280]{1,0:T(8,128)(2,1)} %param.7, bf16[128,1920]{1,0:T(8,128)(2,1)} %bitcast.6, f32[128]{0:T(128)S(1)} %mul.68), kind=kOutput, calls=%fused_computation.4 | convolution fusion | flops 213237760 | bytes 3768832 | tf_op jit(solution)/shard_map/dot_general | solution.py:382
  (155 shorter events, 49.6 us)
Async XLA Ops:
  0.6 40.1 %collective-permute-start.12 = (bf16[640,1280]{1,0:T(8,128)(2,1)}, bf16[640,1280]{1,0:T(8,128)(2,1)}, u32[]{:S(2)}, u32[]{:S(2)}) collective-permute-start(bf16[640,1280]{1,0:T(8,128)(2,1)} %param.7), channel_id=1, source_target_pairs={{0,8},{1,9},{2,10},{3,11},{4,12},{5,13},{6,14},{7,15},{8,0},{9,1},... | collective-permute-start | bytes 4915208 | tf_op jit(solution)/shard_map/ppermute | solution.py:79
  7.4 2.5 collective-permute-start.20
  8.1 48.5 %collective-permute-start.5 = (bf16[640,1280]{1,0:T(8,128)(2,1)}, bf16[640,1280]{1,0:T(8,128)(2,1)}, u32[]{:S(2)}, u32[]{:S(2)}) collective-permute-start(bf16[640,1280]{1,0:T(8,128)(2,1)} %param.7), channel_id=1, source_target_pairs={{0,1},{1,0},{2,3},{3,2},{4,5},{5,4},{6,7},{7,6},{8,9},{9,8},{10,11... | collective-permute-start | bytes 4915208 | tf_op jit(solution)/shard_map/ppermute | solution.py:79
  8.2 33.6 %collective-permute-start.6 = (bf16[384,1280]{1,0:T(8,128)(2,1)}, bf16[384,1280]{1,0:T(8,128)(2,1)}, u32[]{:S(2)}, u32[]{:S(2)}) collective-permute-start(bf16[384,1280]{1,0:T(8,128)(2,1)} %slice.37), channel_id=1, source_target_pairs={{8,16},{9,17},{10,18},{11,19},{12,20},{13,21},{14,22},{15,23},{16,... | collective-permute-start | bytes 2949128 | tf_op jit(solution)/shard_map/ppermute | solution.py:79
  9.9 44.0 %collective-permute-start.21 = (bf16[256,1280]{1,0:T(8,128)(2,1)S(1)}, bf16[256,1280]{1,0:T(8,128)(2,1)}, u32[]{:S(2)}, u32[]{:S(2)}) collective-permute-start(bf16[256,1280]{1,0:T(8,128)(2,1)S(1)} %collective-permute-done.20), channel_id=1, source_target_pairs={{8,0},{9,1},{10,2},{11,3},{12,4},{13,5},{14,6},{15,7},{16,24},{17,... | collective-permute-start | bytes 1966088 | tf_op jit(solution)/shard_map/ppermute | solution.py:79
  13.8 1.4 collective-permute-start.3
  15.1 3.7 %collective-permute-start.4 = (f32[16,256]{1,0:T(8,128)S(1)}, f32[16,256]{1,0:T(8,128)S(1)}, u32[]{:S(2)}, u32[]{:S(2)}) collective-permute-start(f32[16,256]{1,0:T(8,128)S(1)} %add.62), channel_id=1, source_target_pairs={{0,2},{1,3},{2,0},{3,1},{4,6},{5,7},{6,4},{7,5},{8,10},{9,11},{10,... | collective-permute-start | bytes 49160 | tf_op jit(solution)/shard_map/ppermute | solution.py:79
  18.9 72.3 %collective-permute-start = (bf16[1024,1280]{1,0:T(8,128)(2,1)}, bf16[1024,1280]{1,0:T(8,128)(2,1)}, u32[]{:S(2)}, u32[]{:S(2)}) collective-permute-start(bf16[1024,1280]{1,0:T(8,128)(2,1)} %param.5), channel_id=1, source_target_pairs={{1,5},{3,7},{5,1},{7,3},{9,13},{11,15},{13,9},{15,11},{17,21},{19,... | collective-permute-start | bytes 7864328 | tf_op jit(solution)/shard_map/ppermute | solution.py:79
  40.7 54.1 %collective-permute-start.1 = (bf16[1024,1280]{1,0:T(8,128)(2,1)}, bf16[1024,1280]{1,0:T(8,128)(2,1)S(1)}, u32[]{:S(2)}, u32[]{:S(2)}) collective-permute-start(bf16[1024,1280]{1,0:T(8,128)(2,1)} %param.5), channel_id=1, source_target_pairs={{0,1},{1,0},{2,3},{3,2},{4,5},{5,4},{6,7},{7,6},{8,9},{9,8},{10,11... | collective-permute-start | bytes 7864328 | tf_op jit(solution)/shard_map/ppermute | solution.py:79
  41.8 18.8 %copy-start.24 = (bf16[128,1280]{1,0:T(8,128)(2,1)}, bf16[128,1280]{1,0:T(8,128)(2,1)S(1)}, u32[]{:S(2)}) copy-start(bf16[128,1280]{1,0:T(8,128)(2,1)S(1)} %slice.51) | copy-start | bytes 983044
  41.8 53.5 %collective-permute-start.2 = (bf16[1024,1280]{1,0:T(8,128)(2,1)}, bf16[1024,1280]{1,0:T(8,128)(2,1)S(1)}, u32[]{:S(2)}, u32[]{:S(2)}) collective-permute-start(bf16[1024,1280]{1,0:T(8,128)(2,1)} %param.5), channel_id=1, source_target_pairs={{0,5},{2,7},{4,1},{6,3},{8,13},{10,15},{12,9},{14,11},{16,21},{18,... | collective-permute-start | bytes 7864328 | tf_op jit(solution)/shard_map/ppermute | solution.py:79
  53.9 25.0 %collective-permute-start.7 = (bf16[384,1280]{1,0:T(8,128)(2,1)}, bf16[384,1280]{1,0:T(8,128)(2,1)S(1)}, u32[]{:S(2)}, u32[]{:S(2)}) collective-permute-start(bf16[384,1280]{1,0:T(8,128)(2,1)} %collective-permute-done.6), channel_id=1, source_target_pairs={{8,0},{9,1},{10,2},{11,3},{12,4},{13,5},{14,6},{15,7},{16,24},{17,... | collective-permute-start | bytes 2949128 | tf_op jit(solution)/shard_map/ppermute | solution.py:79
  56.6 32.3 %copy-start.16 = (bf16[256,1280]{1,0:T(8,128)(2,1)}, bf16[256,1280]{1,0:T(8,128)(2,1)S(1)}, u32[]{:S(2)}) copy-start(bf16[256,1280]{1,0:T(8,128)(2,1)S(1)} %get-tuple-element.19) | copy-start | bytes 1966084
  56.6 6.0 %collective-permute-start.14 = (bf16[128,1280]{1,0:T(8,128)(2,1)S(1)}, bf16[128,1280]{1,0:T(8,128)(2,1)S(1)}, u32[]{:S(2)}, u32[]{:S(2)}) collective-permute-start(bf16[128,1280]{1,0:T(8,128)(2,1)S(1)} %slice.51), channel_id=1, source_target_pairs={{8,16},{9,17},{10,18},{11,19},{12,20},{13,21},{14,22},{15,23},{16,... | collective-permute-start | bytes 983048 | tf_op jit(solution)/shard_map/ppermute | solution.py:79
  62.6 40.5 %collective-permute-start.22 = (bf16[256,1280]{1,0:T(8,128)(2,1)}, bf16[256,1280]{1,0:T(8,128)(2,1)}, u32[]{:S(2)}, u32[]{:S(2)}) collective-permute-start(bf16[256,1280]{1,0:T(8,128)(2,1)} %broadcast_select_fusion.5), channel_id=1, source_target_pairs={{0,1},{1,0},{2,3},{3,2},{4,5},{5,4},{6,7},{7,6},{8,9},{9,8},{10,11... | collective-permute-start | bytes 1966088 | tf_op jit(solution)/shard_map/ppermute | solution.py:79
  78.9 9.9 %collective-permute-start.15 = (bf16[128,1280]{1,0:T(8,128)(2,1)S(1)}, bf16[128,1280]{1,0:T(8,128)(2,1)S(1)}, u32[]{:S(2)}, u32[]{:S(2)}) collective-permute-start(bf16[128,1280]{1,0:T(8,128)(2,1)S(1)} %collective-permute-done.14), channel_id=1, source_target_pairs={{8,0},{9,1},{10,2},{11,3},{12,4},{13,5},{14,6},{15,7},{16,24},{17,... | collective-permute-start | bytes 983048 | tf_op jit(solution)/shard_map/ppermute | solution.py:79
  88.8 5.9 %collective-permute-start.26 = (bf16[256,1280]{1,0:T(8,128)(2,1)S(1)}, bf16[256,1280]{1,0:T(8,128)(2,1)}, u32[]{:S(2)}, u32[]{:S(2)}) collective-permute-start(bf16[256,1280]{1,0:T(8,128)(2,1)S(1)} %get-tuple-element.19), channel_id=1, source_target_pairs={{8,16},{9,17},{10,18},{11,19},{12,20},{13,21},{14,22},{15,23},{16,... | collective-permute-start | bytes 1966088 | tf_op jit(solution)/shard_map/ppermute | solution.py:79
  91.2 12.1 %collective-permute-start.30 = (bf16[256,1280]{1,0:T(8,128)(2,1)S(1)}, bf16[256,1280]{1,0:T(8,128)(2,1)}, u32[]{:S(2)}, u32[]{:S(2)}) collective-permute-start(bf16[256,1280]{1,0:T(8,128)(2,1)S(1)} %get-tuple-element.20), channel_id=1, source_target_pairs={{8,16},{9,17},{10,18},{11,19},{12,20},{13,21},{14,22},{15,23},{16,... | collective-permute-start | bytes 1966088 | tf_op jit(solution)/shard_map/ppermute | solution.py:79
  94.7 49.4 %collective-permute-start.13 = (bf16[640,1280]{1,0:T(8,128)(2,1)}, bf16[640,1280]{1,0:T(8,128)(2,1)S(1)}, u32[]{:S(2)}, u32[]{:S(2)}) collective-permute-start(bf16[640,1280]{1,0:T(8,128)(2,1)} %collective-permute-done.12), channel_id=1, source_target_pairs={{0,1},{1,0},{2,3},{3,2},{4,5},{5,4},{6,7},{7,6},{8,9},{9,8},{10,11... | collective-permute-start | bytes 4915208 | tf_op jit(solution)/shard_map/ppermute | solution.py:79
  94.8 44.6 %collective-permute-start.8 = (bf16[384,1280]{1,0:T(8,128)(2,1)S(1)}, bf16[384,1280]{1,0:T(8,128)(2,1)}, u32[]{:S(2)}, u32[]{:S(2)}) collective-permute-start(bf16[384,1280]{1,0:T(8,128)(2,1)S(1)} %broadcast_select_fusion.2), channel_id=1, source_target_pairs={{0,1},{1,0},{2,3},{3,2},{4,5},{5,4},{6,7},{7,6},{8,9},{9,8},{10,11... | collective-permute-start | bytes 2949128 | tf_op jit(solution)/shard_map/ppermute | solution.py:79
  95.3 30.7 %collective-permute-start.27 = (bf16[256,1280]{1,0:T(8,128)(2,1)}, bf16[256,1280]{1,0:T(8,128)(2,1)}, u32[]{:S(2)}, u32[]{:S(2)}) collective-permute-start(bf16[256,1280]{1,0:T(8,128)(2,1)} %collective-permute-done.26), channel_id=1, source_target_pairs={{8,0},{9,1},{10,2},{11,3},{12,4},{13,5},{14,6},{15,7},{16,24},{17,... | collective-permute-start | bytes 1966088 | tf_op jit(solution)/shard_map/ppermute | solution.py:79
  103.1 44.1 %collective-permute-start.16 = (bf16[128,1280]{1,0:T(8,128)(2,1)S(1)}, bf16[128,1280]{1,0:T(8,128)(2,1)S(1)}, u32[]{:S(2)}, u32[]{:S(2)}) collective-permute-start(bf16[128,1280]{1,0:T(8,128)(2,1)S(1)} %copy-done.23), channel_id=1, source_target_pairs={{0,1},{1,0},{2,3},{3,2},{4,5},{5,4},{6,7},{7,6},{8,9},{9,8},{10,11... | collective-permute-start | bytes 983048 | tf_op jit(solution)/shard_map/ppermute | solution.py:79
  103.2 36.0 %collective-permute-start.31 = (bf16[256,1280]{1,0:T(8,128)(2,1)}, bf16[256,1280]{1,0:T(8,128)(2,1)S(1)}, u32[]{:S(2)}, u32[]{:S(2)}) collective-permute-start(bf16[256,1280]{1,0:T(8,128)(2,1)} %collective-permute-done.30), channel_id=1, source_target_pairs={{8,0},{9,1},{10,2},{11,3},{12,4},{13,5},{14,6},{15,7},{16,24},{17,... | collective-permute-start | bytes 1966088 | tf_op jit(solution)/shard_map/ppermute | solution.py:79
  107.6 32.4 %copy-start.15 = (bf16[384,1280]{1,0:T(8,128)(2,1)S(1)}, bf16[384,1280]{1,0:T(8,128)(2,1)}, u32[]{:S(2)}) copy-start(bf16[384,1280]{1,0:T(8,128)(2,1)} %copy-done.14) | copy-start | bytes 2949124
  126.0 39.0 %collective-permute-start.23 = (bf16[1024,256]{1,0:T(8,128)(2,1)S(1)}, bf16[1024,256]{1,0:T(8,128)(2,1)S(1)}, u32[]{:S(2)}, u32[]{:S(2)}) collective-permute-start(bf16[1024,256]{1,0:T(8,128)(2,1)S(1)} %get-tuple-element.36), channel_id=1, source_target_pairs={{0,2},{1,3},{2,0},{3,1},{4,6},{5,7},{6,4},{7,5},{8,10},{9,11},{10,... | collective-permute-start | bytes 1572872 | tf_op jit(solution)/shard_map/ppermute | solution.py:79
  139.3 13.6 %collective-permute-start.28 = (bf16[256,1280]{1,0:T(8,128)(2,1)S(1)}, bf16[256,1280]{1,0:T(8,128)(2,1)S(1)}, u32[]{:S(2)}, u32[]{:S(2)}) collective-permute-start(bf16[256,1280]{1,0:T(8,128)(2,1)S(1)} %broadcast_select_fusion.4), channel_id=1, source_target_pairs={{0,1},{1,0},{2,3},{3,2},{4,5},{5,4},{6,7},{7,6},{8,9},{9,8},{10,11... | collective-permute-start | bytes 1966088 | tf_op jit(solution)/shard_map/ppermute | solution.py:79
  139.4 16.3 %collective-permute-start.32 = (bf16[256,1280]{1,0:T(8,128)(2,1)S(1)}, bf16[256,1280]{1,0:T(8,128)(2,1)S(1)}, u32[]{:S(2)}, u32[]{:S(2)}) collective-permute-start(bf16[256,1280]{1,0:T(8,128)(2,1)S(1)} %broadcast_select_fusion.3), channel_id=1, source_target_pairs={{0,1},{1,0},{2,3},{3,2},{4,5},{5,4},{6,7},{7,6},{8,9},{9,8},{10,11... | collective-permute-start | bytes 1966088 | tf_op jit(solution)/shard_map/ppermute | solution.py:79
  144.1 20.5 %collective-permute-start.9 = (bf16[1024,384]{1,0:T(8,128)(2,1)S(1)}, bf16[1024,384]{1,0:T(8,128)(2,1)S(1)}, u32[]{:S(2)}, u32[]{:S(2)}) collective-permute-start(bf16[1024,384]{1,0:T(8,128)(2,1)S(1)} %get-tuple-element.32), channel_id=1, source_target_pairs={{0,2},{1,3},{2,0},{3,1},{4,6},{5,7},{6,4},{7,5},{8,10},{9,11},{10,... | collective-permute-start | bytes 2359304 | tf_op jit(solution)/shard_map/ppermute | solution.py:79
  148.7 21.5 %collective-permute-start.17 = (bf16[1024,128]{1,0:T(8,128)(2,1)S(1)}, bf16[1024,128]{1,0:T(8,128)(2,1)S(1)}, u32[]{:S(2)}, u32[]{:S(2)}) collective-permute-start(bf16[1024,128]{1,0:T(8,128)(2,1)S(1)} %get-tuple-element.34), channel_id=1, source_target_pairs={{0,2},{1,3},{2,0},{3,1},{4,6},{5,7},{6,4},{7,5},{8,10},{9,11},{10,... | collective-permute-start | bytes 786440 | tf_op jit(solution)/shard_map/ppermute | solution.py:79
  154.5 26.9 %collective-permute-start.29 = (bf16[1024,256]{1,0:T(8,128)(2,1)S(1)}, bf16[1024,256]{1,0:T(8,128)(2,1)S(1)}, u32[]{:S(2)}, u32[]{:S(2)}) collective-permute-start(bf16[1024,256]{1,0:T(8,128)(2,1)S(1)} %get-tuple-element.38), channel_id=1, source_target_pairs={{0,2},{1,3},{2,0},{3,1},{4,6},{5,7},{6,4},{7,5},{8,10},{9,11},{10,... | collective-permute-start | bytes 1572872 | tf_op jit(solution)/shard_map/ppermute | solution.py:79
  157.2 34.5 %collective-permute-start.33 = (bf16[1024,256]{1,0:T(8,128)(2,1)S(1)}, bf16[1024,256]{1,0:T(8,128)(2,1)S(1)}, u32[]{:S(2)}, u32[]{:S(2)}) collective-permute-start(bf16[1024,256]{1,0:T(8,128)(2,1)S(1)} %get-tuple-element.40), channel_id=1, source_target_pairs={{0,2},{1,3},{2,0},{3,1},{4,6},{5,7},{6,4},{7,5},{8,10},{9,11},{10,... | collective-permute-start | bytes 1572872 | tf_op jit(solution)/shard_map/ppermute | solution.py:79
  164.9 32.3 %collective-permute-start.10 = (bf16[1024,384]{1,0:T(8,128)(2,1)S(1)}, bf16[1024,384]{1,0:T(8,128)(2,1)S(1)}, u32[]{:S(2)}, u32[]{:S(2)}) collective-permute-start(bf16[1024,384]{1,0:T(8,128)(2,1)S(1)} %add_convert_fusion.refs_1_.refs_0_), channel_id=1, source_target_pairs={{0,1},{1,0},{2,3},{3,2},{4,5},{5,4},{6,7},{7,6},{8,9},{9,8},{10,11... | collective-permute-start | bytes 2359304 | tf_op jit(solution)/shard_map/ppermute | solution.py:79
  165.2 27.5 %copy-start.6 = (bf16[1024,256]{1,0:T(8,128)(2,1)}, bf16[1024,256]{1,0:T(8,128)(2,1)S(1)}, u32[]{:S(2)}) copy-start(bf16[1024,256]{1,0:T(8,128)(2,1)S(1)} %add_convert_fusion.3.refs_0_) | copy-start | bytes 1572868
  165.2 27.5 %collective-permute-start.24 = (bf16[1024,256]{1,0:T(8,128)(2,1)S(1)}, bf16[1024,256]{1,0:T(8,128)(2,1)S(1)}, u32[]{:S(2)}, u32[]{:S(2)}) collective-permute-start(bf16[1024,256]{1,0:T(8,128)(2,1)S(1)} %add_convert_fusion.3.refs_0_), channel_id=1, source_target_pairs={{0,1},{1,0},{2,3},{3,2},{4,5},{5,4},{6,7},{7,6},{8,9},{9,8},{10,11... | collective-permute-start | bytes 1572872 | tf_op jit(solution)/shard_map/ppermute | solution.py:79
  170.2 24.0 %collective-permute-start.25 = (bf16[1024,256]{1,0:T(8,128)(2,1)S(1)}, bf16[1024,256]{1,0:T(8,128)(2,1)S(1)}, u32[]{:S(2)}, u32[]{:S(2)}) collective-permute-start(bf16[1024,256]{1,0:T(8,128)(2,1)S(1)} %add_convert_fusion.3.refs_0_), channel_id=1, source_target_pairs={{1,4},{3,6},{5,0},{7,2},{9,13},{11,14},{13,9},{15,10},{17,21},{19,... | collective-permute-start | bytes 1572872 | tf_op jit(solution)/shard_map/ppermute | solution.py:79
  181.4 18.0 %collective-permute-start.11 = (bf16[1024,384]{1,0:T(8,128)(2,1)S(1)}, bf16[1024,384]{1,0:T(8,128)(2,1)S(1)}, u32[]{:S(2)}, u32[]{:S(2)}) collective-permute-start(bf16[1024,384]{1,0:T(8,128)(2,1)S(1)} %add_convert_fusion.refs_1_.refs_0_), channel_id=1, source_target_pairs={{1,4},{3,6},{5,0},{7,2},{9,13},{11,14},{13,9},{15,10},{17,21},{19,... | collective-permute-start | bytes 2359304 | tf_op jit(solution)/shard_map/ppermute | solution.py:79
  191.7 9.4 %collective-permute-start.34 = (bf16[1024,256]{1,0:T(8,128)(2,1)}, bf16[1024,256]{1,0:T(8,128)(2,1)S(1)}, u32[]{:S(2)}, u32[]{:S(2)}) collective-permute-start(bf16[1024,256]{1,0:T(8,128)(2,1)} %add_convert_fusion.2.refs_6_), channel_id=1, source_target_pairs={{0,1},{1,0},{2,3},{3,2},{4,5},{5,4},{6,7},{7,6},{8,9},{9,8},{10,11... | collective-permute-start | bytes 1572872 | tf_op jit(solution)/shard_map/ppermute | solution.py:79
  192.7 17.5 %collective-permute-start.36 = (bf16[1024,256]{1,0:T(8,128)(2,1)}, bf16[1024,256]{1,0:T(8,128)(2,1)}, u32[]{:S(2)}, u32[]{:S(2)}) collective-permute-start(bf16[1024,256]{1,0:T(8,128)(2,1)} %add_convert_fusion.2.refs_6_), channel_id=1, source_target_pairs={{1,5},{3,7},{5,1},{7,3},{9,12},{11,15},{13,8},{15,11},{17,20},{19,... | collective-permute-start | bytes 1572872 | tf_op jit(solution)/shard_map/ppermute | solution.py:79
  195.0 15.2 %collective-permute-start.35 = (bf16[1024,256]{1,0:T(8,128)(2,1)}, bf16[1024,256]{1,0:T(8,128)(2,1)}, u32[]{:S(2)}, u32[]{:S(2)}) collective-permute-start(bf16[1024,256]{1,0:T(8,128)(2,1)} %add_convert_fusion.1.refs_7_), channel_id=1, source_target_pairs={{0,1},{1,0},{2,3},{3,2},{4,5},{5,4},{6,7},{7,6},{8,9},{9,8},{10,11... | collective-permute-start | bytes 1572872 | tf_op jit(solution)/shard_map/ppermute | solution.py:79
  197.2 13.1 %collective-permute-start.37 = (bf16[1024,256]{1,0:T(8,128)(2,1)}, bf16[1024,256]{1,0:T(8,128)(2,1)}, u32[]{:S(2)}, u32[]{:S(2)}) collective-permute-start(bf16[1024,256]{1,0:T(8,128)(2,1)} %add_convert_fusion.1.refs_7_), channel_id=1, source_target_pairs={{1,5},{3,7},{5,1},{7,3},{9,12},{11,15},{13,8},{15,11},{17,20},{19,... | collective-permute-start | bytes 1572872 | tf_op jit(solution)/shard_map/ppermute | solution.py:79
  200.3 23.2 %collective-permute-start.18 = (bf16[1024,128]{1,0:T(8,128)(2,1)}, bf16[1024,128]{1,0:T(8,128)(2,1)}, u32[]{:S(2)}, u32[]{:S(2)}) collective-permute-start(bf16[1024,128]{1,0:T(8,128)(2,1)} %add_convert_fusion.4.refs_3_), channel_id=1, source_target_pairs={{0,1},{1,0},{2,3},{3,2},{4,5},{5,4},{6,7},{7,6},{8,9},{9,8},{10,11... | collective-permute-start | bytes 786440 | tf_op jit(solution)/shard_map/ppermute | solution.py:79
  201.8 21.7 %collective-permute-start.19 = (bf16[1024,128]{1,0:T(8,128)(2,1)}, bf16[1024,128]{1,0:T(8,128)(2,1)}, u32[]{:S(2)}, u32[]{:S(2)}) collective-permute-start(bf16[1024,128]{1,0:T(8,128)(2,1)} %add_convert_fusion.4.refs_3_), channel_id=1, source_target_pairs={{1,5},{3,7},{5,1},{7,3},{9,12},{11,15},{13,8},{15,11},{17,20},{19,... | collective-permute-start | bytes 786440 | tf_op jit(solution)/shard_map/ppermute | solution.py:79
  203.3 43.9 %all-to-all-start = ((bf16[8,16,1920]{2,1,0:T(8,128)(2,1)}), bf16[8,16,1920]{2,1,0:T(8,128)(2,1)}, u32[]{:S(2)}, u32[]{:S(2)}) async-start(bf16[8,16,1920]{2,1,0:T(8,128)(2,1)} %pad_maximum_fusion.1), calls=%async_computation | async-start | bytes 983040 | tf_op jit(solution)/shard_map/all_to_all | solution.py:324
  226.7 2.9 %collective-permute-start.38 = (f32[32]{0:T(128)S(1)}, f32[32]{0:T(128)S(1)}, u32[]{:S(2)}, u32[]{:S(2)}) collective-permute-start(f32[32]{0:T(128)S(1)} %compare_select_fusion), channel_id=1, source_target_pairs={{0,1},{1,0},{2,3},{3,2},{4,5},{5,4},{6,7},{7,6},{8,9},{9,8},{10,11... | collective-permute-start | bytes 392 | tf_op jit(solution)/shard_map/ppermute | solution.py:79
  229.6 3.6 %collective-permute-start.39 = (f32[32]{0:T(128)S(1)}, f32[32]{0:T(128)S(1)}, u32[]{:S(2)}, u32[]{:S(2)}) collective-permute-start(f32[32]{0:T(128)S(1)} %fusion.74), channel_id=1, source_target_pairs={{0,2},{1,3},{2,0},{3,1},{4,6},{5,7},{6,4},{7,5},{8,10},{9,11},{10,... | collective-permute-start | bytes 392 | tf_op jit(solution)/shard_map/ppermute | solution.py:79
  233.2 3.6 %collective-permute-start.40 = (f32[32]{0:T(128)S(1)}, f32[32]{0:T(128)S(1)}, u32[]{:S(2)}, u32[]{:S(2)}) collective-permute-start(f32[32]{0:T(128)S(1)} %add.72), channel_id=1, source_target_pairs={{0,4},{1,5},{2,6},{3,7},{4,0},{5,1},{6,2},{7,3},{8,12},{9,13},{10,... | collective-permute-start | bytes 392 | tf_op jit(solution)/shard_map/ppermute | solution.py:79
  236.8 3.6 %collective-permute-start.41 = (f32[32]{0:T(128)S(1)}, f32[32]{0:T(128)S(1)}, u32[]{:S(2)}, u32[]{:S(2)}) collective-permute-start(f32[32]{0:T(128)S(1)} %add.73), channel_id=1, source_target_pairs={{0,8},{1,9},{2,10},{3,11},{4,12},{5,13},{6,14},{7,15},{8,0},{9,1},... | collective-permute-start | bytes 392 | tf_op jit(solution)/shard_map/ppermute | solution.py:79
  240.4 5.4 %collective-permute-start.42 = (f32[32]{0:T(128)S(1)}, f32[32]{0:T(128)S(1)}, u32[]{:S(2)}, u32[]{:S(2)}) collective-permute-start(f32[32]{0:T(128)S(1)} %add.74), channel_id=1, source_target_pairs={{0,24},{1,25},{2,26},{3,27},{4,28},{5,29},{6,30},{7,31},{8,16},{9,... | collective-permute-start | bytes 392 | tf_op jit(solution)/shard_map/ppermute | solution.py:79
  (24 other events, 114.0 us)
